TPU v7x, 32 devices: a whole 2x2x4 slice. The times are simulated.
32 devices in a mesh: blk: 8 (over y, x, core), ulysses: 4 (over z).
Axes of the slice: x: 2, y: 2, z: 4, core: 2. Of those that a mesh axis runs over, the one named last changes fastest.
Arguments:
- tokens: bfloat16 [2048, 3072], P(('blk', 'ulysses')), may hold values from -6 to 6
- mod_shift: float32 [3072], replicated, may hold values from -3 to 3
- mod_scale: float32 [3072], replicated, may hold values from -3 to 3
- mod_gate: float32 [3072], replicated, may hold values from 0.5 to 1.5
- qkv_weight: bfloat16 [3, 3072, 3072], P(None, None, 'ulysses'), may hold values from -0.109375 to 0.109375
- query_gain: float32 [128], replicated, may hold values from 1 to 16
- key_gain: float32 [128], replicated, may hold values from 1 to 16
- out_weight: bfloat16 [3072, 3072], P(None, 'ulysses'), may hold values from -0.109375 to 0.109375
Outputs:
- mixed: bfloat16 [2048, 3072], P(('blk', 'ulysses'))
All inputs are finite; a program needn't handle non-finite values.
Results may differ from a plain program's by a relative error of at most 0.013.
The roundings to bfloat16 on the way count: a program that leaves them out, or rounds other values in their place, can miss the bound.
Values may be sent and summed in bfloat16 or wider, within the bound.
A program may use at most 128 MiB of HBM per device.

v0:
```python
import functools
import math

import jax
import jax.numpy as jnp
from jax import lax
from jax.experimental import pallas as pl
from jax.experimental.pallas import tpu as pltpu
from jax.sharding import PartitionSpec as P

MESH = pl.DeviceIdType.MESH
BF = jnp.bfloat16
F32 = jnp.float32


def highest_bit(mask):
    return 1 << (mask.bit_length() - 1)


def lowest_bit(mask):
    return mask & -mask


def source_slot(mask, part):
    if mask & 1:
        return mask - 1, 1
    bit = highest_bit(mask) if part == 0 else lowest_bit(mask)
    return mask - bit, bit


def kernel(
    n_u, n_blk,
    tok_ref, shift_ref, scale_ref, gate_ref, w_hbm, qg_ref, kg_ref, wo_hbm, out_ref,
    w_ref, wo_ref, mod, q_ref, kv, att, stage, br,
    w_sem, sa_r, sa_l, ra, sb, rb, sc_r, sc_l, rc, sd, rd,
):
    z = lax.axis_index("ulysses")
    b = lax.axis_index("blk")
    rows, model = tok_ref.shape
    head = qg_ref.shape[1]
    width = w_ref.shape[2]
    heads = width // head
    factor = 1.0 / math.sqrt(head)
    last = n_u - 1
    half = rows // 2
    bits = [1 << i for i in range(n_blk.bit_length() - 1)]
    pair = 2 if heads % 2 == 0 else heads
    tile = pair * head

    for j in (1, 2, 0):
        pltpu.make_async_copy(w_hbm.at[j], w_ref.at[j], w_sem.at[j]).start()
    pltpu.make_async_copy(wo_hbm, wo_ref, w_sem.at[3]).start()

    def flip(bit):
        return b + (1 - 2 * ((b // bit) % 2)) * bit

    barrier = pltpu.get_barrier_semaphore()
    for d in range(1, n_u):
        pl.semaphore_signal(
            barrier, inc=1, device_id={"ulysses": (z + d) % n_u}, device_id_type=MESH
        )
    for bit in bits:
        pl.semaphore_signal(barrier, inc=1, device_id={"blk": flip(bit)}, device_id_type=MESH)

    wide = tok_ref[...].astype(F32)
    center = jnp.mean(wide, axis=-1, keepdims=True)
    spread = jnp.mean((wide - center) ** 2, axis=-1, keepdims=True)
    normed = (wide - center) * lax.rsqrt(spread + 1e-06)
    modulated = (normed * (1.0 + scale_ref[...]) + shift_ref[...]).astype(BF)
    mod[pl.ds(2 * z, 2)] = modulated.reshape(2, half, model)

    pl.semaphore_wait(barrier, n_u - 1 + len(bits))

    def line_copy(buf, index, send, recv, step):
        return pltpu.make_async_remote_copy(
            src_ref=buf.at[index], dst_ref=buf.at[index],
            send_sem=send.at[index], recv_sem=recv.at[index],
            device_id={"ulysses": z + step}, device_id_type=MESH,
        )

    def a_right(o):
        return line_copy(mod, o, sa_r, ra, 1)

    def a_left(o):
        return line_copy(mod, o, sa_l, ra, -1)

    def b_copy(mask, part, s):
        slot, bit = source_slot(mask, part)
        return pltpu.make_async_remote_copy(
            src_ref=kv.at[part, :, slot, s], dst_ref=kv.at[part, :, mask, s],
            send_sem=sb.at[mask, part, s], recv_sem=rb.at[mask, part, s],
            device_id={"blk": flip(bit)}, device_id_type=MESH,
        )

    masks = range(1, n_blk)

    def b_send(slot, part, s):
        for mask in sorted(masks, key=lambda m: m & 1):
            if source_slot(mask, part)[0] == slot:
                b_copy(mask, part, s).start()

    def b_level(level, s):
        for part in (0, 1):
            for mask in masks:
                if mask % 2 == 0 and bin(mask).count("1") == level:
                    b_copy(mask, part, s).wait_recv()
                    b_send(mask, part, s)

    levels = range(1, len(bits))

    def head_norm(sums, gain, scale):
        meansq = jnp.mean(sums * sums, axis=-1, keepdims=True)
        return sums * lax.rsqrt(meansq + 1e-06) * gain * scale

    def project(j, first, count, put):
        def body(i, _):
            start = pl.multiple_of(i * tile, tile)
            sums = jnp.dot(
                mod[pl.ds(first, count)].reshape(count * half, model),
                w_ref[j, :, pl.ds(start, tile)],
                preferred_element_type=F32,
            )
            for e in range(pair):
                put(i * pair + e, sums[:, e * head:(e + 1) * head])
            return 0

        lax.fori_loop(0, heads // pair, body, 0)

    def project_chunk(first, count, own=False):
        units = pl.ds(first, count)

        def ready(j):
            if own:
                pltpu.make_async_copy(w_hbm.at[j], w_ref.at[j], w_sem.at[j]).wait()

        def put_key(h, sums):
            keys = head_norm(sums, kg_ref[...], 1.0).astype(BF)
            kv[0, h, 0, units] = keys.reshape(count, half, head)

        def put_value(h, sums):
            kv[1, h, 0, units] = sums.astype(BF).reshape(count, half, head)

        def put_query(h, sums):
            queries = head_norm(sums, qg_ref[...], factor).astype(BF)
            q_ref[h, units] = queries.reshape(count, half, head)

        ready(1)
        project(1, first, count, put_key)
        for u in range(count):
            b_send(0, 0, first + u)
        ready(2)
        project(2, first, count, put_value)
        for u in range(count):
            b_send(0, 1, first + u)
        ready(0)
        project(0, first, count, put_query)

    for u in range(2):
        @pl.when(z < last)
        def _():
            a_right(2 * z + u).start()

        @pl.when(z > 0)
        def _():
            a_left(2 * z + u).start()

    project_chunk(2 * z, 2, own=True)

    def at_distance(k, act):
        for side in (-1, 1):
            o = z + side * k

            @pl.when((o >= 0) & (o <= last))
            def _():
                act(o)

    def pass_levels(which):
        def act(o):
            for level in which:
                for u in range(2):
                    b_level(level, 2 * o + u)
        return act

    def receive(k):
        for u in range(2):
            @pl.when(z - k >= 0)
            def _():
                a_right(2 * (z - k) + u).wait_recv()

                @pl.when(z < last)
                def _():
                    a_right(2 * (z - k) + u).start()

            @pl.when(z + k <= last)
            def _():
                a_left(2 * (z + k) + u).wait_recv()

                @pl.when(z > 0)
                def _():
                    a_left(2 * (z + k) + u).start()

    def previous(k, which):
        if isinstance(k, int) and k == 1:
            pass_levels(which)(z)
        else:
            at_distance(k - 1, pass_levels(which))

    for k in range(1, last):
        receive(k)
        previous(k, levels[:1])
        at_distance(k, lambda o: project_chunk(2 * o, 2))
        previous(k, levels[1:])

    ends = (z == 0) | (z == last)
    far = last - z

    def far_half(u):
        @pl.when(ends)
        def _():
            @pl.when(z == 0)
            def _():
                a_left(2 * far + u).wait_recv()

            @pl.when(z > 0)
            def _():
                a_right(2 * far + u).wait_recv()

            project_chunk(2 * far + u, 1)

    def far_levels(u, which):
        @pl.when(ends)
        def _():
            for level in which:
                b_level(level, 2 * far + u)

    previous(last, levels[:1])
    far_half(0)
    previous(last, levels[1:])
    far_levels(0, levels[:1])
    far_half(1)
    far_levels(0, levels[1:])
    far_levels(1, levels)

    def b_finish(s, _):
        for part in (0, 1):
            for mask in masks:
                if mask % 2 == 1:
                    b_copy(mask, part, s).wait_recv()
        return 0

    lax.fori_loop(0, 2 * n_u, b_finish, 0)
    pltpu.make_async_copy(wo_hbm, wo_ref, w_sem.at[3]).wait()

    keys_all = n_blk * n_u * rows

    def order(i):
        return jnp.where(i % 2 == 0, i // 2, last - i // 2)

    def c_right(o, src):
        return pltpu.make_async_remote_copy(
            src_ref=att.at[o, src], dst_ref=att.at[o, src],
            send_sem=sc_r.at[o, src], recv_sem=rc.at[o, src],
            device_id={"ulysses": z + 1}, device_id_type=MESH,
        )

    def c_left(o, src):
        return pltpu.make_async_remote_copy(
            src_ref=att.at[o, src], dst_ref=att.at[o, src],
            send_sem=sc_l.at[o, src], recv_sem=rc.at[o, src],
            device_id={"ulysses": z - 1}, device_id_type=MESH,
        )

    def d_copy(o, src):
        return pltpu.make_async_remote_copy(
            src_ref=stage.at[o], dst_ref=br.at[src],
            send_sem=sd.at[o], recv_sem=rd.at[src],
            device_id={"ulysses": o}, device_id_type=MESH,
        )

    group = 2 if n_u % 2 == 0 else 1

    def attend(chunks):
        for h in range(heads):
            keys = kv[0, h].reshape(keys_all, head)
            values = kv[1, h].reshape(keys_all, head)
            queries = jnp.concatenate(
                [q_ref[h, pl.ds(2 * o, 2)].reshape(rows, head) for o in chunks], axis=0
            )
            scores = lax.dot_general(
                queries, keys, (((1,), (1,)), ((), ())), preferred_element_type=F32
            )
            powers = jnp.exp(scores - jnp.max(scores, axis=-1, keepdims=True))
            total = jnp.sum(powers, axis=-1, keepdims=True)
            numerator = jnp.dot(powers.astype(BF), values, preferred_element_type=F32)
            result = (numerator / total).astype(BF)
            for g, o in enumerate(chunks):
                att[o, z, :, h * head:(h + 1) * head] = result[g * rows:(g + 1) * rows]

    def pass_right(o, src):
        c_right(o, src).wait_recv()

        @pl.when(z < last)
        def _():
            c_right(o, src).start()

    def pass_left(o, src):
        c_left(o, src).wait_recv()

        @pl.when(z > 0)
        def _():
            c_left(o, src).start()

    low = z < n_u // 2

    def attend_step(t, _):
        @pl.when(t < n_u // group)
        def _():
            chunks = [order(group * t + g) for g in range(group)]
            attend(chunks)
            for o in chunks:
                @pl.when(z < last)
                def _():
                    c_right(o, z).start()

                @pl.when(z > 0)
                def _():
                    c_left(o, z).start()

        for g in range(group):
            @pl.when((t > 0) & low & (z > 0))
            def _():
                pass_left(order(group * (t - 1) + g), z + 1)

            @pl.when((t > 0) & jnp.logical_not(low) & (z < last))
            def _():
                pass_right(order(group * (t - 1) + g), z - 1)

        return 0

    lax.fori_loop(0, n_u // group + 1, attend_step, 0)

    def mix_step(t, _):
        for k in range(last, 0, -1):
            i = t - k + 1
            held = (i >= 0) & (i < n_u)
            right_too = held & (z - k >= 0)
            left_too = held & (z + k <= last)
            if k == 1:
                right_too = right_too & (low | (z == last))
                left_too = left_too & (jnp.logical_not(low) | (z == 0))

            @pl.when(right_too)
            def _():
                pass_right(order(i), z - k)

            @pl.when(left_too)
            def _():
                pass_left(order(i), z + k)

        @pl.when(t >= last - 1)
        def _():
            o = order(t - last + 1)
            total = jnp.zeros((rows, width), F32)
            for src in range(n_u):
                total += jnp.dot(
                    att[o, src], wo_ref[src * width:(src + 1) * width, :],
                    preferred_element_type=F32,
                )

            @pl.when(o == z)
            def _():
                br[z] = total.astype(BF)

            @pl.when(o != z)
            def _():
                stage[o] = total.astype(BF)
                d_copy(o, z).start()

        return 0

    lax.fori_loop(0, n_u + last - 1, mix_step, 0)

    for src in range(n_u):
        @pl.when(src != z)
        def _():
            d_copy(src, src).wait_recv()

        cols = slice(src * width, (src + 1) * width)
        out_ref[:, cols] = (
            tok_ref[:, cols].astype(F32) + gate_ref[:, cols] * br[src].astype(F32)
        ).astype(BF)

    def finish(s, _):
        for u in range(2):
            @pl.when((s <= z) & (z < last))
            def _():
                a_right(2 * s + u).wait_send()

            @pl.when((s >= z) & (z > 0))
            def _():
                a_left(2 * s + u).wait_send()

        for src in range(n_u):
            @pl.when((src <= z) & (z < last))
            def _():
                c_right(s, src).wait_send()

            @pl.when((src >= z) & (z > 0))
            def _():
                c_left(s, src).wait_send()

        @pl.when(s != z)
        def _():
            d_copy(s, z).wait_send()

        for part in (0, 1):
            for mask in masks:
                for u in range(2):
                    b_copy(mask, part, 2 * s + u).wait_send()
        return 0

    lax.fori_loop(0, n_u, finish, 0)


def local(n_u, n_blk, tokens, mod_shift, mod_scale, mod_gate, qkv_weight, query_gain, key_gain, out_weight):
    rows, model = tokens.shape
    width = qkv_weight.shape[2]
    head = query_gain.shape[0]
    heads = width // head
    vmem = pl.BlockSpec(memory_space=pltpu.VMEM)
    hbm = pl.BlockSpec(memory_space=pl.ANY)
    dma = pltpu.SemaphoreType.DMA
    return pl.pallas_call(
        functools.partial(kernel, n_u, n_blk),
        out_shape=jax.ShapeDtypeStruct((rows, model), BF),
        in_specs=[vmem, vmem, vmem, vmem, hbm, vmem, vmem, hbm],
        out_specs=vmem,
        scratch_shapes=[
            pltpu.VMEM(qkv_weight.shape, BF),
            pltpu.VMEM(out_weight.shape, BF),
            pltpu.VMEM((2 * n_u, rows // 2, model), BF),
            pltpu.VMEM((heads, 2 * n_u, rows // 2, head), BF),
            pltpu.VMEM((2, heads, n_blk, 2 * n_u, rows // 2, head), BF),
            pltpu.VMEM((n_u, n_u, rows, width), BF),
            pltpu.VMEM((n_u, rows, width), BF),
            pltpu.VMEM((n_u, rows, width), BF),
            dma((4,)),
            dma((2 * n_u,)), dma((2 * n_u,)), dma((2 * n_u,)),
            dma((n_blk, 2, 2 * n_u)), dma((n_blk, 2, 2 * n_u)),
            dma((n_u, n_u)), dma((n_u, n_u)), dma((n_u, n_u)),
            dma((n_u,)), dma((n_u,)),
        ],
        compiler_params=pltpu.CompilerParams(
            collective_id=0, has_side_effects=True, vmem_limit_bytes=66_000_000
        ),
    )(
        tokens, mod_shift[None], mod_scale[None], mod_gate[None],
        qkv_weight, query_gain[None], key_gain[None], out_weight,
    )


def solution(mesh):
    in_specs = (
        P(("blk", "ulysses"), None), P(), P(), P(),
        P(None, None, "ulysses"), P(), P(), P(None, "ulysses"),
    )
    out_specs = P(("blk", "ulysses"), None)
    body = functools.partial(local, mesh.shape["ulysses"], mesh.shape["blk"])
    return jax.shard_map(body, mesh=mesh, in_specs=in_specs, out_specs=out_specs, check_vma=False)
```

profile of v0, /device:TPU:0, one launch (start us, length us, event | category | flops | bytes accessed | tf_op | source)
XLA Modules:
  0.0 88.2 jit_solution(15057531912933960203)
XLA Ops:
  0.0 86.4 %shard_map.82 = bf16[64,3072]{1,0:T(8,128)(2,1)} custom-call(bf16[64,3072]{1,0:T(8,128)(2,1)} %tok_ref.1, f32[1,3072]{1,0:T(1,128)} %bitcast.5, f32[1,3072]{1,0:T(1,128)} %bitcast.6, f32[1,3072]{1,0:T(1,128)} %bitcast.7, bf16[3,3072,768]{2,1,0:T(8,128)(2,1)} %w_hbm.1, f32[1,128]{1,0:T(1,128)} %bitcast.8, f32[1,128]{1,0:T(1,128)} %bitcast.9, ...), custom_call_target="tpu_custom_call" | custom-call | tf_op jit(solution)/shard_map/pallas_call | solution.py:433
  86.4 1.8 %copy.10 = bf16[64,3072]{1,0:T(8,128)(2,1)} copy(bf16[64,3072]{1,0:T(8,128)(2,1)} %shard_map.82) | data formatting | bytes 786432
where the time goes:
time: 88.4 us; the launch traced here: 88.2 us
  Pallas kernels  86.4 us (98%)
  local copies, waits for them, and re-layouts  1.77 us (2%)
    pallas_call x1, Pallas kernels, local(): pl.pallas_call(functools.partial(kernel, n_u, n_blk), out_shape=jax.Shape...  86.4 us

commit v1 on v0

--- a/solution.py
+++ b/solution.py
@@ -11,6 +11,7 @@
 MESH = pl.DeviceIdType.MESH
 BF = jnp.bfloat16
 F32 = jnp.float32
+SPLIT = 2
 
 
 def highest_bit(mask):
@@ -422,6 +423,471 @@
     lax.fori_loop(0, n_u, finish, 0)
 
 
+def split_kernel(
+    n_u, n_blk,
+    tok_ref, shift_ref, scale_ref, gate_ref, w_hbm, qg_ref, kg_ref, wo_hbm, out_ref,
+    w_ref, wo_ref, mod, q_ref, kv, att, xatt, stage, br,
+    w_sem, sa_r, sa_l, ra, sb, rb, sq, rq, sx, rx, sc_r, sc_l, rc, sd, rd,
+):
+    z = lax.axis_index("ulysses")
+    b = lax.axis_index("blk")
+    rows, model = tok_ref.shape
+    head = qg_ref.shape[1]
+    width = w_ref.shape[2]
+    heads = width // head
+    share = heads // 2
+    cols = share * head
+    factor = 1.0 / math.sqrt(head)
+    last = n_u - 1
+    half = rows // 2
+    bits = [1 << i for i in range(n_blk.bit_length() - 1)]
+    masks = range(1, n_blk)
+    side = (b // SPLIT) % 2
+    mine = side * share
+    theirs = (1 - side) * share
+
+    for j in (1, 2, 0):
+        pltpu.make_async_copy(w_hbm.at[j], w_ref.at[j], w_sem.at[j]).start()
+    pltpu.make_async_copy(wo_hbm, wo_ref, w_sem.at[3]).start()
+
+    def flip(bit):
+        return b + (1 - 2 * ((b // bit) % 2)) * bit
+
+    barrier = pltpu.get_barrier_semaphore()
+    for d in range(1, n_u):
+        pl.semaphore_signal(
+            barrier, inc=1, device_id={"ulysses": (z + d) % n_u}, device_id_type=MESH
+        )
+    for bit in bits:
+        pl.semaphore_signal(barrier, inc=1, device_id={"blk": flip(bit)}, device_id_type=MESH)
+
+    wide = tok_ref[...].astype(F32)
+    center = jnp.mean(wide, axis=-1, keepdims=True)
+    spread = jnp.mean((wide - center) ** 2, axis=-1, keepdims=True)
+    normed = (wide - center) * lax.rsqrt(spread + 1e-06)
+    modulated = (normed * (1.0 + scale_ref[...]) + shift_ref[...]).astype(BF)
+    mod[pl.ds(2 * z, 2)] = modulated.reshape(2, half, model)
+
+    with jax.named_scope("barrier"):
+        pl.semaphore_wait(barrier, n_u - 1 + len(bits))
+
+    def line_copy(buf, index, send, recv, step):
+        return pltpu.make_async_remote_copy(
+            src_ref=buf.at[index], dst_ref=buf.at[index],
+            send_sem=send.at[index], recv_sem=recv.at[index],
+            device_id={"ulysses": z + step}, device_id_type=MESH,
+        )
+
+    def a_right(o):
+        return line_copy(mod, o, sa_r, ra, 1)
+
+    def a_left(o):
+        return line_copy(mod, o, sa_l, ra, -1)
+
+    def source(mask, part):
+        if mask & 1:
+            return mask - 1, 1
+        if mask == SPLIT:
+            return 0, SPLIT
+        rest = mask & ~SPLIT
+        bit = highest_bit(rest) if part == 0 else lowest_bit(rest)
+        return mask - bit, bit
+
+    def b_copy(mask, part, u):
+        slot, bit = source(mask, part)
+        own = pl.ds(theirs if bit == SPLIT else mine, share)
+        return pltpu.make_async_remote_copy(
+            src_ref=kv.at[part, own, slot, u], dst_ref=kv.at[part, own, mask, u],
+            send_sem=sb.at[mask, part, u], recv_sem=rb.at[mask, part, u],
+            device_id={"blk": flip(bit)}, device_id_type=MESH,
+        )
+
+    def b_wait(mask, part, u):
+        here = kv.at[part, pl.ds(mine, share), mask, u]
+        pltpu.make_async_remote_copy(
+            src_ref=here, dst_ref=here,
+            send_sem=sb.at[mask, part, u], recv_sem=rb.at[mask, part, u],
+            device_id={"blk": flip(source(mask, part)[1])}, device_id_type=MESH,
+        ).wait_recv()
+
+    def q_copy(u, first):
+        heads_of = pl.ds(first, share)
+        return pltpu.make_async_remote_copy(
+            src_ref=q_ref.at[heads_of, 0, u], dst_ref=q_ref.at[heads_of, 1, u],
+            send_sem=sq.at[u], recv_sem=rq.at[u],
+            device_id={"blk": flip(SPLIT)}, device_id_type=MESH,
+        )
+
+    def b_send(slot, part, u):
+        for mask in sorted(masks, key=lambda m: (m & 1, m != SPLIT)):
+            if source(mask, part)[0] == slot:
+                b_copy(mask, part, u).start()
+
+    def depth_of(mask):
+        return bin(mask).count("1")
+
+    def b_level(level, u, parts=(0, 1)):
+        for part in parts:
+            for mask in masks:
+                if mask % 2 == 0 and depth_of(mask) == level:
+                    b_wait(mask, part, u)
+                    b_send(mask, part, u)
+
+    depth = len(bits) - 1
+
+    def level_one(o):
+        for u in range(2):
+            b_level(1, 2 * o + u)
+
+    def level_rest(o):
+        for level in range(2, depth + 1):
+            for u in range(2):
+                b_level(level, 2 * o + u)
+
+    def head_norm(sums, gain, scale):
+        meansq = jnp.mean(sums * sums, axis=-1, keepdims=True)
+        return sums * lax.rsqrt(meansq + 1e-06) * gain * scale
+
+    def project_chunk(first, count, own=False, between=None):
+        units = pl.ds(first, count)
+
+        def sums_of(j):
+            if own:
+                pltpu.make_async_copy(w_hbm.at[j], w_ref.at[j], w_sem.at[j]).wait()
+            sums = jnp.dot(
+                mod[units].reshape(count * half, model), w_ref[j], preferred_element_type=F32
+            )
+            return [sums[:, h * head:(h + 1) * head] for h in range(heads)]
+
+        for h, sums in enumerate(sums_of(1)):
+            keys = head_norm(sums, kg_ref[...], 1.0).astype(BF)
+            kv[0, h, 0, units] = keys.reshape(count, half, head)
+        for u in range(count):
+            b_send(0, 0, first + u)
+        for h, sums in enumerate(sums_of(2)):
+            kv[1, h, 0, units] = sums.astype(BF).reshape(count, half, head)
+        for u in range(count):
+            b_send(0, 1, first + u)
+        if between is not None:
+            between()
+        for h, sums in enumerate(sums_of(0)):
+            queries = head_norm(sums, qg_ref[...], factor).astype(BF)
+            q_ref[h, 0, units] = queries.reshape(count, half, head)
+        for u in range(count):
+            q_copy(first + u, theirs).start()
+
+    def whole_chunk(o):
+        project_chunk(2 * o, 2)
+
+    for u in range(2):
+        @pl.when(z < last)
+        def _():
+            a_right(2 * z + u).start()
+
+        @pl.when(z > 0)
+        def _():
+            a_left(2 * z + u).start()
+
+    def receive(k, u):
+        @pl.when(z - k >= 0)
+        def _():
+            a_right(2 * (z - k) + u).wait_recv()
+
+            @pl.when(z < last)
+            def _():
+                a_right(2 * (z - k) + u).start()
+
+        @pl.when(z + k <= last)
+        def _():
+            a_left(2 * (z + k) + u).wait_recv()
+
+            @pl.when(z > 0)
+            def _():
+                a_left(2 * (z + k) + u).start()
+
+    def at_first(k, act):
+        o = jnp.where(z >= k, z - k, z + k)
+
+        @pl.when((z >= k) | (z + k <= last))
+        def _():
+            act(o)
+
+    def at_second(k, act):
+        @pl.when((z >= k) & (z + k <= last) & (k > 0))
+        def _():
+            act(z + k)
+
+    with jax.named_scope("own"):
+        project_chunk(2 * z, 2, own=True)
+    receive(1, 0)
+    if last > 1:
+        receive(1, 1)
+
+    def line_step(k, _):
+        at_first(k - 1, level_one)
+        at_first(k, whole_chunk)
+        receive(k + 1, 0)
+        at_second(k - 1, level_one)
+        at_first(k - 1, level_rest)
+        at_second(k, whole_chunk)
+
+        @pl.when(k + 1 < last)
+        def _():
+            receive(k + 1, 1)
+
+        at_second(k - 1, level_rest)
+        return 0
+
+    with jax.named_scope("line"):
+        lax.fori_loop(1, last, line_step, 0)
+
+    ends = (z == 0) | (z == last)
+    far = last - z
+
+    with jax.named_scope("far"):
+        at_first(last - 1, level_one)
+
+        def far_step(u, _):
+            @pl.when(ends)
+            def _():
+                @pl.when(u == 1)
+                def _():
+                    receive(last, 1)
+
+                def between():
+                    @pl.when(u == 1)
+                    def _():
+                        b_level(1, 2 * far)
+
+                project_chunk(2 * far + u, 1, between=between)
+
+            @pl.when(u == 0)
+            def _():
+                at_second(last - 1, level_one)
+                at_first(last - 1, level_rest)
+                at_second(last - 1, level_rest)
+            return 0
+
+        lax.fori_loop(0, 2, far_step, 0)
+
+        @pl.when(ends)
+        def _():
+            b_level(1, 2 * far + 1)
+            for level in range(2, depth + 1):
+                b_level(level, 2 * far)
+                b_level(level, 2 * far + 1)
+
+    def b_finish(u, _):
+        for part in (0, 1):
+            for mask in masks:
+                if mask % 2 == 1:
+                    b_wait(mask, part, u)
+        q_copy(u, mine).wait_recv()
+        return 0
+
+    with jax.named_scope("b_finish"):
+        lax.fori_loop(0, 2 * n_u, b_finish, 0)
+        pltpu.make_async_copy(wo_hbm, wo_ref, w_sem.at[3]).wait()
+
+    keys_all = n_blk * n_u * rows
+
+    def order(i):
+        return jnp.where(i % 2 == 0, i // 2, last - i // 2)
+
+    def c_copy(o, src, sd, send, step):
+        ref = att.at[o, src, :, pl.ds(pl.multiple_of(sd * cols, head), cols)]
+        return pltpu.make_async_remote_copy(
+            src_ref=ref, dst_ref=ref,
+            send_sem=send.at[o, src, sd], recv_sem=rc.at[o, src, sd],
+            device_id={"ulysses": z + step}, device_id_type=MESH,
+        )
+
+    def c_right(o, src, sd):
+        return c_copy(o, src, sd, sc_r, 1)
+
+    def c_left(o, src, sd):
+        return c_copy(o, src, sd, sc_l, -1)
+
+    def c_both(o, sd):
+        @pl.when(z < last)
+        def _():
+            c_right(o, z, sd).start()
+
+        @pl.when(z > 0)
+        def _():
+            c_left(o, z, sd).start()
+
+    def x_copy(o, sd):
+        return pltpu.make_async_remote_copy(
+            src_ref=xatt.at[o],
+            dst_ref=att.at[o, z, :, pl.ds(pl.multiple_of(sd * cols, head), cols)],
+            send_sem=sx.at[o], recv_sem=rx.at[o],
+            device_id={"blk": flip(SPLIT)}, device_id_type=MESH,
+        )
+
+    def d_copy(o, src):
+        return pltpu.make_async_remote_copy(
+            src_ref=stage.at[o], dst_ref=br.at[src],
+            send_sem=sd.at[o], recv_sem=rd.at[src],
+            device_id={"ulysses": o}, device_id_type=MESH,
+        )
+
+    def attend(o):
+        chunk = pl.ds(2 * o, 2)
+        for r in range(share):
+            h = mine + r
+            keys = kv[0, h].reshape(keys_all, head)
+            values = kv[1, h].reshape(keys_all, head)
+            queries = jnp.concatenate(
+                [q_ref[h, p, chunk].reshape(rows, head) for p in range(2)], axis=0
+            )
+            scores = lax.dot_general(
+                queries, keys, (((1,), (1,)), ((), ())), preferred_element_type=F32
+            )
+            powers = jnp.exp(scores - jnp.max(scores, axis=-1, keepdims=True))
+            total = jnp.sum(powers, axis=-1, keepdims=True)
+            numerator = jnp.dot(powers.astype(BF), values, preferred_element_type=F32)
+            result = (numerator / total).astype(BF)
+            place = pl.ds(pl.multiple_of(side * cols + r * head, head), head)
+            att[o, z, :, place] = result[:rows]
+            xatt[o, :, r * head:(r + 1) * head] = result[rows:]
+
+    def pass_right(o, src):
+        for sd in (side, 1 - side):
+            c_right(o, src, sd).wait_recv()
+
+            @pl.when(z < last)
+            def _():
+                c_right(o, src, sd).start()
+
+    def pass_left(o, src):
+        for sd in (side, 1 - side):
+            c_left(o, src, sd).wait_recv()
+
+            @pl.when(z > 0)
+            def _():
+                c_left(o, src, sd).start()
+
+    low = z < n_u // 2
+
+    def attend_step(t, _):
+        @pl.when(t < n_u)
+        def _():
+            o = order(t)
+            with jax.named_scope("attend"):
+                attend(o)
+            c_both(o, side)
+            x_copy(o, side).start()
+
+        @pl.when((t > 0) & (t <= n_u))
+        def _():
+            o = order(t - 1)
+            x_copy(o, 1 - side).wait_recv()
+            c_both(o, 1 - side)
+
+        @pl.when((t > 1) & low & (z > 0))
+        def _():
+            pass_left(order(t - 2), z + 1)
+
+        @pl.when((t > 1) & jnp.logical_not(low) & (z < last))
+        def _():
+            pass_right(order(t - 2), z - 1)
+
+        return 0
+
+    with jax.named_scope("attend_loop"):
+        lax.fori_loop(0, n_u + 2, attend_step, 0)
+
+    def mix_step(t, _):
+        for k in range(last, 0, -1):
+            i = t - k + 1
+            held = (i >= 0) & (i < n_u)
+            right_too = held & (z - k >= 0)
+            left_too = held & (z + k <= last)
+            if k == 1:
+                right_too = right_too & (low | (z == last))
+                left_too = left_too & (jnp.logical_not(low) | (z == 0))
+
+            @pl.when(right_too)
+            def _():
+                pass_right(order(i), z - k)
+
+            @pl.when(left_too)
+            def _():
+                pass_left(order(i), z + k)
+
+        @pl.when(t >= last - 1)
+        def _():
+            o = order(t - last + 1)
+            total = jnp.zeros((rows, width), F32)
+            for src in range(n_u):
+                total += jnp.dot(
+                    att[o, src], wo_ref[src * width:(src + 1) * width, :],
+                    preferred_element_type=F32,
+                )
+
+            @pl.when(o == z)
+            def _():
+                br[z] = total.astype(BF)
+
+            @pl.when(o != z)
+            def _():
+                stage[o] = total.astype(BF)
+                d_copy(o, z).start()
+
+        return 0
+
+    with jax.named_scope("mix_loop"):
+        lax.fori_loop(0, n_u + last - 1, mix_step, 0)
+
+    with jax.named_scope("final"):
+        for src in range(n_u):
+            @pl.when(src != z)
+            def _():
+                d_copy(src, src).wait_recv()
+
+            at = slice(src * width, (src + 1) * width)
+            out_ref[:, at] = (
+                tok_ref[:, at].astype(F32) + gate_ref[:, at] * br[src].astype(F32)
+            ).astype(BF)
+
+    def finish(s, _):
+        for u in range(2):
+            @pl.when((s <= z) & (z < last))
+            def _():
+                a_right(2 * s + u).wait_send()
+
+            @pl.when((s >= z) & (z > 0))
+            def _():
+                a_left(2 * s + u).wait_send()
+
+        for src in range(n_u):
+            for sd_of in range(2):
+                @pl.when((src <= z) & (z < last))
+                def _():
+                    c_right(s, src, sd_of).wait_send()
+
+                @pl.when((src >= z) & (z > 0))
+                def _():
+                    c_left(s, src, sd_of).wait_send()
+
+        @pl.when(s != z)
+        def _():
+            d_copy(s, z).wait_send()
+
+        x_copy(s, side).wait_send()
+        for u in range(2):
+            q_copy(2 * s + u, theirs).wait_send()
+        for part in (0, 1):
+            for mask in masks:
+                for u in range(2):
+                    b_copy(mask, part, 2 * s + u).wait_send()
+        return 0
+
+    with jax.named_scope("finish"):
+        lax.fori_loop(0, n_u, finish, 0)
+
+
 def local(n_u, n_blk, tokens, mod_shift, mod_scale, mod_gate, qkv_weight, query_gain, key_gain, out_weight):
     rows, model = tokens.shape
     width = qkv_weight.shape[2]
@@ -430,26 +896,42 @@
     vmem = pl.BlockSpec(memory_space=pltpu.VMEM)
     hbm = pl.BlockSpec(memory_space=pl.ANY)
     dma = pltpu.SemaphoreType.DMA
+    split = heads % 2 == 0 and n_blk % (2 * SPLIT) == 0
+    buffers = [
+        pltpu.VMEM(qkv_weight.shape, BF),
+        pltpu.VMEM(out_weight.shape, BF),
+        pltpu.VMEM((2 * n_u, rows // 2, model), BF),
+    ]
+    line_sems = [dma((4,)), dma((2 * n_u,)), dma((2 * n_u,)), dma((2 * n_u,))]
+    block_sems = [dma((n_blk, 2, 2 * n_u)), dma((n_blk, 2, 2 * n_u))]
+    keys = pltpu.VMEM((2, heads, n_blk, 2 * n_u, rows // 2, head), BF)
+    attended = pltpu.VMEM((n_u, n_u, rows, width), BF)
+    mixed = pltpu.VMEM((n_u, rows, width), BF)
+    if split:
+        body = split_kernel
+        scratch = buffers + [
+            pltpu.VMEM((heads, 2, 2 * n_u, rows // 2, head), BF), keys,
+            attended, pltpu.VMEM((n_u, rows, width // 2), BF), mixed, mixed,
+        ] + line_sems + block_sems + [
+            dma((2 * n_u,)), dma((2 * n_u,)), dma((n_u,)), dma((n_u,)),
+            dma((n_u, n_u, 2)), dma((n_u, n_u, 2)), dma((n_u, n_u, 2)),
+            dma((n_u,)), dma((n_u,)),
+        ]
+    else:
+        body = kernel
+        scratch = buffers + [
+            pltpu.VMEM((heads, 2 * n_u, rows // 2, head), BF), keys,
+            attended, mixed, mixed,
+        ] + line_sems + block_sems + [
+            dma((n_u, n_u)), dma((n_u, n_u)), dma((n_u, n_u)),
+            dma((n_u,)), dma((n_u,)),
+        ]
     return pl.pallas_call(
-        functools.partial(kernel, n_u, n_blk),
+        functools.partial(body, n_u, n_blk),
         out_shape=jax.ShapeDtypeStruct((rows, model), BF),
         in_specs=[vmem, vmem, vmem, vmem, hbm, vmem, vmem, hbm],
         out_specs=vmem,
-        scratch_shapes=[
-            pltpu.VMEM(qkv_weight.shape, BF),
-            pltpu.VMEM(out_weight.shape, BF),
-            pltpu.VMEM((2 * n_u, rows // 2, model), BF),
-            pltpu.VMEM((heads, 2 * n_u, rows // 2, head), BF),
-            pltpu.VMEM((2, heads, n_blk, 2 * n_u, rows // 2, head), BF),
-            pltpu.VMEM((n_u, n_u, rows, width), BF),
-            pltpu.VMEM((n_u, rows, width), BF),
-            pltpu.VMEM((n_u, rows, width), BF),
-            dma((4,)),
-            dma((2 * n_u,)), dma((2 * n_u,)), dma((2 * n_u,)),
-            dma((n_blk, 2, 2 * n_u)), dma((n_blk, 2, 2 * n_u)),
-            dma((n_u, n_u)), dma((n_u, n_u)), dma((n_u, n_u)),
-            dma((n_u,)), dma((n_u,)),
-        ],
+        scratch_shapes=scratch,
         compiler_params=pltpu.CompilerParams(
             collective_id=0, has_side_effects=True, vmem_limit_bytes=66_000_000
         ),

time: 88.4 us -> 83.1 us (0.940)
  Pallas kernels: 86.4 us -> 81 us
    pallas_call x1, Pallas kernels: 86.4 us -> 81 us  [local(): pl.pallas_call(functools.partial(body, n_u, n_blk), out_shape=jax.ShapeDt...]
where the time goes in v1:
time: 83.1 us; the launch traced here: 82.8 us
  Pallas kernels  81 us (97%)
  local copies, waits for them, and re-layouts  1.77 us (2%)
    pallas_call x1, Pallas kernels, local(): pl.pallas_call(functools.partial(body, n_u, n_blk), out_shape=jax.ShapeDt...  81 us
    unnamed x1, local copies, waits for them, and re-layouts  1.77 us

profile of v1, /device:TPU:0, one launch (start us, length us, event | category | flops | bytes accessed | tf_op | source)
XLA Modules:
  0.0 82.8 jit_solution(3520754749862526926)
XLA Ops:
  0.0 81.0 %shard_map.82 = bf16[64,3072]{1,0:T(8,128)(2,1)} custom-call(bf16[64,3072]{1,0:T(8,128)(2,1)} %tok_ref.1, f32[1,3072]{1,0:T(1,128)} %bitcast.5, f32[1,3072]{1,0:T(1,128)} %bitcast.6, f32[1,3072]{1,0:T(1,128)} %bitcast.7, bf16[3,3072,768]{2,1,0:T(8,128)(2,1)} %w_hbm.1, f32[1,128]{1,0:T(1,128)} %bitcast.8, f32[1,128]{1,0:T(1,128)} %bitcast.9, ...), custom_call_target="tpu_custom_call" | custom-call | tf_op jit(solution)/shard_map/pallas_call | solution.py:929
  81.0 1.8 %copy.10 = bf16[64,3072]{1,0:T(8,128)(2,1)} copy(bf16[64,3072]{1,0:T(8,128)(2,1)} %shard_map.82) | data formatting | bytes 786432

commit v2 on v1

--- a/solution.py
+++ b/solution.py
@@ -425,8 +425,9 @@
 
 def split_kernel(
     n_u, n_blk,
-    tok_ref, shift_ref, scale_ref, gate_ref, w_hbm, qg_ref, kg_ref, wo_hbm, out_ref,
-    w_ref, wo_ref, mod, q_ref, kv, att, xatt, stage, br,
+    tok_hbm, shift_hbm, scale_hbm, gate_hbm, w_hbm, qg_ref, kg_ref, wo_hbm, out_ref,
+    w_ref, wo_ref, mod, q_ref, kv, att, xatt, pair_ref, stage, br,
+    tok_ref, shift_ref, scale_ref, gate_ref, in_sem,
     w_sem, sa_r, sa_l, ra, sb, rb, sq, rq, sx, rx, sc_r, sc_l, rc, sd, rd,
 ):
     z = lax.axis_index("ulysses")
@@ -446,10 +447,6 @@
     mine = side * share
     theirs = (1 - side) * share
 
-    for j in (1, 2, 0):
-        pltpu.make_async_copy(w_hbm.at[j], w_ref.at[j], w_sem.at[j]).start()
-    pltpu.make_async_copy(wo_hbm, wo_ref, w_sem.at[3]).start()
-
     def flip(bit):
         return b + (1 - 2 * ((b // bit) % 2)) * bit
 
@@ -460,6 +457,20 @@
         )
     for bit in bits:
         pl.semaphore_signal(barrier, inc=1, device_id={"blk": flip(bit)}, device_id_type=MESH)
+
+    inputs = [
+        pltpu.make_async_copy(src, dst, in_sem.at[i])
+        for i, (src, dst) in enumerate((
+            (tok_hbm, tok_ref), (shift_hbm, shift_ref), (scale_hbm, scale_ref), (gate_hbm, gate_ref),
+        ))
+    ]
+    for copy in inputs:
+        copy.start()
+    for copy in inputs:
+        copy.wait()
+    for j in (1, 2, 0):
+        pltpu.make_async_copy(w_hbm.at[j], w_ref.at[j], w_sem.at[j]).start()
+    pltpu.make_async_copy(wo_hbm, wo_ref, w_sem.at[3]).start()
 
     wide = tok_ref[...].astype(F32)
     center = jnp.mean(wide, axis=-1, keepdims=True)
@@ -548,36 +559,44 @@
         meansq = jnp.mean(sums * sums, axis=-1, keepdims=True)
         return sums * lax.rsqrt(meansq + 1e-06) * gain * scale
 
-    def project_chunk(first, count, own=False, between=None):
-        units = pl.ds(first, count)
+    def project(starts, count, own=False, between=None):
+        size = count * half
 
         def sums_of(j):
             if own:
                 pltpu.make_async_copy(w_hbm.at[j], w_ref.at[j], w_sem.at[j]).wait()
+            tokens = [mod[pl.ds(first, count)].reshape(size, model) for first in starts]
             sums = jnp.dot(
-                mod[units].reshape(count * half, model), w_ref[j], preferred_element_type=F32
+                jnp.concatenate(tokens, axis=0), w_ref[j], preferred_element_type=F32
             )
             return [sums[:, h * head:(h + 1) * head] for h in range(heads)]
 
+        def put(value, at):
+            for i, first in enumerate(starts):
+                at(pl.ds(first, count), value[i * size:(i + 1) * size].reshape(count, half, head))
+
+        def send(act):
+            for first in starts:
+                for u in range(count):
+                    act(first + u)
+
         for h, sums in enumerate(sums_of(1)):
-            keys = head_norm(sums, kg_ref[...], 1.0).astype(BF)
-            kv[0, h, 0, units] = keys.reshape(count, half, head)
-        for u in range(count):
-            b_send(0, 0, first + u)
+            def put_keys(units, part):
+                kv[0, h, 0, units] = part
+            put(head_norm(sums, kg_ref[...], 1.0).astype(BF), put_keys)
+        send(lambda u: b_send(0, 0, u))
         for h, sums in enumerate(sums_of(2)):
-            kv[1, h, 0, units] = sums.astype(BF).reshape(count, half, head)
-        for u in range(count):
-            b_send(0, 1, first + u)
+            def put_values(units, part):
+                kv[1, h, 0, units] = part
+            put(sums.astype(BF), put_values)
+        send(lambda u: b_send(0, 1, u))
         if between is not None:
             between()
         for h, sums in enumerate(sums_of(0)):
-            queries = head_norm(sums, qg_ref[...], factor).astype(BF)
-            q_ref[h, 0, units] = queries.reshape(count, half, head)
-        for u in range(count):
-            q_copy(first + u, theirs).start()
-
-    def whole_chunk(o):
-        project_chunk(2 * o, 2)
+            def put_queries(units, part):
+                q_ref[h, 0, units] = part
+            put(head_norm(sums, qg_ref[...], factor).astype(BF), put_queries)
+        send(lambda u: q_copy(u, theirs).start())
 
     for u in range(2):
         @pl.when(z < last)
@@ -605,37 +624,43 @@
             def _():
                 a_left(2 * (z + k) + u).start()
 
-    def at_first(k, act):
-        o = jnp.where(z >= k, z - k, z + k)
-
-        @pl.when((z >= k) | (z + k <= last))
-        def _():
-            act(o)
-
-    def at_second(k, act):
-        @pl.when((z >= k) & (z + k <= last) & (k > 0))
+    def at_each(k, act):
+        @pl.when(z >= k)
+        def _():
+            act(z - k)
+
+        @pl.when((z + k <= last) & (k > 0))
         def _():
             act(z + k)
 
+    def project_at(k, between):
+        two = (z >= k) & (z + k <= last)
+
+        @pl.when(two)
+        def _():
+            project([2 * (z - k), 2 * (z + k)], 2, between=between)
+
+        @pl.when(jnp.logical_not(two) & ((z >= k) | (z + k <= last)))
+        def _():
+            project([2 * jnp.where(z >= k, z - k, z + k)], 2, between=between)
+
     with jax.named_scope("own"):
-        project_chunk(2 * z, 2, own=True)
+        project([2 * z], 2, own=True)
     receive(1, 0)
+    level_one(z)
     if last > 1:
         receive(1, 1)
 
     def line_step(k, _):
-        at_first(k - 1, level_one)
-        at_first(k, whole_chunk)
+        with jax.named_scope("project"):
+            project_at(k, lambda: at_each(k - 1, level_rest))
         receive(k + 1, 0)
-        at_second(k - 1, level_one)
-        at_first(k - 1, level_rest)
-        at_second(k, whole_chunk)
+        at_each(k, level_one)
 
         @pl.when(k + 1 < last)
         def _():
             receive(k + 1, 1)
 
-        at_second(k - 1, level_rest)
         return 0
 
     with jax.named_scope("line"):
@@ -645,33 +670,31 @@
     far = last - z
 
     with jax.named_scope("far"):
-        at_first(last - 1, level_one)
+        @pl.when(jnp.logical_not(ends))
+        def _():
+            at_each(last - 1, level_rest)
 
         def far_step(u, _):
-            @pl.when(ends)
-            def _():
+            @pl.when(u == 1)
+            def _():
+                receive(last, 1)
+
+            def between():
+                @pl.when(u == 0)
+                def _():
+                    at_each(last - 1, level_rest)
+
                 @pl.when(u == 1)
                 def _():
-                    receive(last, 1)
-
-                def between():
-                    @pl.when(u == 1)
-                    def _():
-                        b_level(1, 2 * far)
-
-                project_chunk(2 * far + u, 1, between=between)
-
-            @pl.when(u == 0)
-            def _():
-                at_second(last - 1, level_one)
-                at_first(last - 1, level_rest)
-                at_second(last - 1, level_rest)
+                    b_level(1, 2 * far)
+
+            with jax.named_scope("project_half"):
+                project([2 * far + u], 1, between=between)
             return 0
 
-        lax.fori_loop(0, 2, far_step, 0)
-
         @pl.when(ends)
         def _():
+            lax.fori_loop(0, 2, far_step, 0)
             b_level(1, 2 * far + 1)
             for level in range(2, depth + 1):
                 b_level(level, 2 * far)
@@ -691,8 +714,10 @@
 
     keys_all = n_blk * n_u * rows
 
-    def order(i):
-        return jnp.where(i % 2 == 0, i // 2, last - i // 2)
+    def order(i, rightward):
+        inner = n_u - 2
+        low_end = (i == inner) == rightward
+        return jnp.where(i < inner, i + 1, jnp.where(low_end, 0, last))
 
     def c_copy(o, src, sd, send, step):
         ref = att.at[o, src, :, pl.ds(pl.multiple_of(sd * cols, head), cols)]
@@ -708,14 +733,29 @@
     def c_left(o, src, sd):
         return c_copy(o, src, sd, sc_l, -1)
 
-    def c_both(o, sd):
-        @pl.when(z < last)
-        def _():
-            c_right(o, z, sd).start()
-
-        @pl.when(z > 0)
-        def _():
-            c_left(o, z, sd).start()
+    low = z < n_u // 2
+
+    def c_send(t, sd):
+        o = order(t, low)
+
+        def start(right, chunk):
+            @pl.when(right & (z < last))
+            def _():
+                c_right(chunk, z, sd).start()
+
+            @pl.when(jnp.logical_not(right) & (z > 0))
+            def _():
+                c_left(chunk, z, sd).start()
+
+        start(low, o)
+
+        @pl.when(t != n_u - 2)
+        def _():
+            start(jnp.logical_not(low), o)
+
+        @pl.when(t == n_u - 1)
+        def _():
+            start(jnp.logical_not(low), order(t - 1, low))
 
     def x_copy(o, sd):
         return pltpu.make_async_remote_copy(
@@ -732,93 +772,96 @@
             device_id={"ulysses": o}, device_id_type=MESH,
         )
 
-    def attend(o):
-        chunk = pl.ds(2 * o, 2)
+    def attend(t):
+        first, second = t == 0, t == n_u - 1
+        groups = (
+            (first, order(jnp.where(first, 0, t - 1), low)),
+            (jnp.logical_not(second), order(jnp.where(second, t, t + 1), low)),
+        )
         for r in range(share):
             h = mine + r
             keys = kv[0, h].reshape(keys_all, head)
             values = kv[1, h].reshape(keys_all, head)
-            queries = jnp.concatenate(
-                [q_ref[h, p, chunk].reshape(rows, head) for p in range(2)], axis=0
-            )
+            queries = jnp.concatenate([
+                q_ref[h, jnp.where(away, 1, 0), pl.ds(2 * o, 2)].reshape(rows, head)
+                for away, o in groups
+            ], axis=0)
             scores = lax.dot_general(
                 queries, keys, (((1,), (1,)), ((), ())), preferred_element_type=F32
             )
             powers = jnp.exp(scores - jnp.max(scores, axis=-1, keepdims=True))
             total = jnp.sum(powers, axis=-1, keepdims=True)
             numerator = jnp.dot(powers.astype(BF), values, preferred_element_type=F32)
-            result = (numerator / total).astype(BF)
-            place = pl.ds(pl.multiple_of(side * cols + r * head, head), head)
-            att[o, z, :, place] = result[:rows]
-            xatt[o, :, r * head:(r + 1) * head] = result[rows:]
-
-    def pass_right(o, src):
-        for sd in (side, 1 - side):
-            c_right(o, src, sd).wait_recv()
-
-            @pl.when(z < last)
-            def _():
-                c_right(o, src, sd).start()
-
-    def pass_left(o, src):
-        for sd in (side, 1 - side):
-            c_left(o, src, sd).wait_recv()
-
-            @pl.when(z > 0)
-            def _():
-                c_left(o, src, sd).start()
-
-    low = z < n_u // 2
+            pair_ref[:, r * head:(r + 1) * head] = (numerator / total).astype(BF)
+        for g, (away, o) in enumerate(groups):
+            @pl.when(away)
+            def _():
+                xatt[o] = pair_ref[g * rows:(g + 1) * rows]
+                x_copy(o, side).start()
+
+            @pl.when(jnp.logical_not(away))
+            def _():
+                place = pl.ds(pl.multiple_of(side * cols, head), cols)
+                att[o, z, :, place] = pair_ref[g * rows:(g + 1) * rows]
+
+        @pl.when(t > 0)
+        def _():
+            c_send(t - 1, side)
+
+        @pl.when(second)
+        def _():
+            c_send(t, side)
+
+    def pass_on(right, o, src, sd):
+        copy = c_right(o, src, sd) if right else c_left(o, src, sd)
+        copy.wait_recv()
+
+        @pl.when((z < last) if right else (z > 0))
+        def _():
+            copy.start()
+
+    def pass_when(when, right, i, src):
+        @pl.when(when & (i >= 0) & (i < n_u))
+        def _():
+            pass_on(right, order(i, right), src, side)
+
+        @pl.when(when & (i >= 1) & (i <= n_u))
+        def _():
+            pass_on(right, order(i - 1, right), src, 1 - side)
+
+    def x_step(t):
+        x_copy(order(t, low), 1 - side).wait_recv()
+        c_send(t, 1 - side)
 
     def attend_step(t, _):
-        @pl.when(t < n_u)
-        def _():
-            o = order(t)
-            with jax.named_scope("attend"):
-                attend(o)
-            c_both(o, side)
-            x_copy(o, side).start()
-
-        @pl.when((t > 0) & (t <= n_u))
-        def _():
-            o = order(t - 1)
-            x_copy(o, 1 - side).wait_recv()
-            c_both(o, 1 - side)
-
-        @pl.when((t > 1) & low & (z > 0))
-        def _():
-            pass_left(order(t - 2), z + 1)
-
-        @pl.when((t > 1) & jnp.logical_not(low) & (z < last))
-        def _():
-            pass_right(order(t - 2), z - 1)
+        with jax.named_scope("attend"):
+            attend(t)
+
+        @pl.when(t > 1)
+        def _():
+            x_step(t - 2)
 
         return 0
 
     with jax.named_scope("attend_loop"):
-        lax.fori_loop(0, n_u + 2, attend_step, 0)
-
-    def mix_step(t, _):
-        for k in range(last, 0, -1):
-            i = t - k + 1
-            held = (i >= 0) & (i < n_u)
-            right_too = held & (z - k >= 0)
-            left_too = held & (z + k <= last)
-            if k == 1:
-                right_too = right_too & (low | (z == last))
-                left_too = left_too & (jnp.logical_not(low) | (z == 0))
-
-            @pl.when(right_too)
-            def _():
-                pass_right(order(i), z - k)
-
-            @pl.when(left_too)
-            def _():
-                pass_left(order(i), z + k)
-
-        @pl.when(t >= last - 1)
-        def _():
-            o = order(t - last + 1)
+        lax.fori_loop(0, n_u, attend_step, 0)
+        for t in range(max(n_u - 2, 0), n_u):
+            x_step(t)
+
+    def near_step(i, _):
+        pass_when(low & (z > 0), False, i, z + 1)
+        pass_when(jnp.logical_not(low) & (z < last), True, i, z - 1)
+        return 0
+
+    with jax.named_scope("near_loop"):
+        lax.fori_loop(0, n_u + 1, near_step, 0)
+
+    gap = 2
+    reach = jnp.where(ends, last, jnp.maximum(z, last - z))
+
+    def mix(i, _):
+        o = order(i, jnp.logical_not(low))
+        with jax.named_scope("mix"):
             total = jnp.zeros((rows, width), F32)
             for src in range(n_u):
                 total += jnp.dot(
@@ -826,19 +869,35 @@
                     preferred_element_type=F32,
                 )
 
-            @pl.when(o == z)
-            def _():
-                br[z] = total.astype(BF)
-
-            @pl.when(o != z)
-            def _():
-                stage[o] = total.astype(BF)
-                d_copy(o, z).start()
+        @pl.when(o == z)
+        def _():
+            br[z] = total.astype(BF)
+
+        @pl.when(o != z)
+        def _():
+            stage[o] = total.astype(BF)
+            d_copy(o, z).start()
 
         return 0
 
+    def mix_step(t, _):
+        for k in range(1, last + 1):
+            i = t - gap * (k - 1)
+            if k == 1:
+                pass_when((z >= k) & (low | (z == last)), True, i, z - k)
+                pass_when((z + k <= last) & (jnp.logical_not(low) | (z == 0)), False, i, z + k)
+            else:
+                pass_when(z >= k, True, i, z - k)
+                pass_when(z + k <= last, False, i, z + k)
+
+        i = t - gap * (reach - 1) - 1
+        held = (i >= 0) & (i < n_u) & (ends | (i != n_u - 2))
+        both = jnp.logical_not(ends) & (i == n_u - 1)
+        lax.fori_loop(jnp.where(both, i - 1, i), jnp.where(held, i + 1, i), mix, 0)
+        return 0
+
     with jax.named_scope("mix_loop"):
-        lax.fori_loop(0, n_u + last - 1, mix_step, 0)
+        lax.fori_loop(0, n_u + gap * (last - 1) + 1, mix_step, 0)
 
     with jax.named_scope("final"):
         for src in range(n_u):
@@ -907,11 +966,15 @@
     keys = pltpu.VMEM((2, heads, n_blk, 2 * n_u, rows // 2, head), BF)
     attended = pltpu.VMEM((n_u, n_u, rows, width), BF)
     mixed = pltpu.VMEM((n_u, rows, width), BF)
+    row = pltpu.VMEM((1, model), F32)
+    early = hbm if split else vmem
     if split:
         body = split_kernel
         scratch = buffers + [
             pltpu.VMEM((heads, 2, 2 * n_u, rows // 2, head), BF), keys,
-            attended, pltpu.VMEM((n_u, rows, width // 2), BF), mixed, mixed,
+            attended, pltpu.VMEM((n_u, rows, width // 2), BF),
+            pltpu.VMEM((2 * rows, width // 2), BF), mixed, mixed,
+            pltpu.VMEM((rows, model), BF), row, row, row, dma((4,)),
         ] + line_sems + block_sems + [
             dma((2 * n_u,)), dma((2 * n_u,)), dma((n_u,)), dma((n_u,)),
             dma((n_u, n_u, 2)), dma((n_u, n_u, 2)), dma((n_u, n_u, 2)),
@@ -929,7 +992,7 @@
     return pl.pallas_call(
         functools.partial(body, n_u, n_blk),
         out_shape=jax.ShapeDtypeStruct((rows, model), BF),
-        in_specs=[vmem, vmem, vmem, vmem, hbm, vmem, vmem, hbm],
+        in_specs=[early, early, early, early, hbm, vmem, vmem, hbm],
         out_specs=vmem,
         scratch_shapes=scratch,
         compiler_params=pltpu.CompilerParams(

time: 83.1 us -> 80.3 us (0.966)
  Pallas kernels: 81 us -> 78.3 us
    pallas_call x1, Pallas kernels: 81 us -> 78.3 us  [local(): pl.pallas_call(functools.partial(body, n_u, n_blk), out_shape=jax.ShapeDt...]
where the time goes in v2:
time: 80.3 us; the launch traced here: 80.1 us
  Pallas kernels  78.3 us (98%)
  local copies, waits for them, and re-layouts  1.77 us (2%)
    pallas_call x1, Pallas kernels, local(): pl.pallas_call(functools.partial(body, n_u, n_blk), out_shape=jax.ShapeDt...  78.3 us
    unnamed x1, local copies, waits for them, and re-layouts  1.77 us

profile of v2, /device:TPU:0, one launch (start us, length us, event | category | flops | bytes accessed | tf_op | source)
XLA Modules:
  0.0 80.1 jit_solution(7866474073325590450)
XLA Ops:
  0.0 78.3 %shard_map.82 = bf16[64,3072]{1,0:T(8,128)(2,1)} custom-call(bf16[64,3072]{1,0:T(8,128)(2,1)} %tok_hbm.1, f32[1,3072]{1,0:T(1,128)} %bitcast.5, f32[1,3072]{1,0:T(1,128)} %bitcast.6, f32[1,3072]{1,0:T(1,128)} %bitcast.7, bf16[3,3072,768]{2,1,0:T(8,128)(2,1)} %w_hbm.1, f32[1,128]{1,0:T(1,128)} %bitcast.8, f32[1,128]{1,0:T(1,128)} %bitcast.9, ...), custom_call_target="tpu_custom_call" | custom-call | tf_op jit(solution)/shard_map/pallas_call | solution.py:992
  78.3 1.8 %copy.10 = bf16[64,3072]{1,0:T(8,128)(2,1)} copy(bf16[64,3072]{1,0:T(8,128)(2,1)} %shard_map.82) | data formatting | bytes 786432

commit v3 on v2

--- a/solution.py
+++ b/solution.py
@@ -426,9 +426,9 @@
 def split_kernel(
     n_u, n_blk,
     tok_hbm, shift_hbm, scale_hbm, gate_hbm, w_hbm, qg_ref, kg_ref, wo_hbm, out_ref,
-    w_ref, wo_ref, mod, q_ref, kv, att, xatt, pair_ref, stage, br,
-    tok_ref, shift_ref, scale_ref, gate_ref, in_sem,
-    w_sem, sa_r, sa_l, ra, sb, rb, sq, rq, sx, rx, sc_r, sc_l, rc, sd, rd,
+    w_ref, wo_ref, mod, q_ref, kv, wx_ref, att, xatt, pair_ref, stage, br,
+    tok_ref, shift_ref, scale_ref, gate_ref, in_sem, swz, rwz, sw, rw, rw_core,
+    w_sem, sa_r, sa_l, ra, sb, rb, rb_core, sq, rq, sx, rx, sc, rc, sd, rd,
 ):
     z = lax.axis_index("ulysses")
     b = lax.axis_index("blk")
@@ -446,6 +446,14 @@
     side = (b // SPLIT) % 2
     mine = side * share
     theirs = (1 - side) * share
+    line_half = n_u // 2
+    low = z < line_half
+    hub = jnp.where(low, line_half - 1, line_half)
+    is_hub = z == hub
+    onward = jnp.where(low, 1, -1)
+    away = jnp.where(low, hub - z, z - hub)
+    slice_rows = model // n_blk
+    part_rows = slice_rows // 2
 
     def flip(bit):
         return b + (1 - 2 * ((b // bit) % 2)) * bit
@@ -468,9 +476,21 @@
         copy.start()
     for copy in inputs:
         copy.wait()
+    own_slice = pl.ds(pl.multiple_of(b * slice_rows, 16), slice_rows)
+    wo_slice = pltpu.make_async_copy(wo_hbm.at[own_slice], wo_ref.at[own_slice], w_sem.at[3])
+    wo_whole = pltpu.make_async_copy(wo_hbm, wo_ref, w_sem.at[3])
+
+    @pl.when(jnp.logical_not(is_hub))
+    def _():
+        wo_slice.start()
+
     for j in (1, 2, 0):
         pltpu.make_async_copy(w_hbm.at[j], w_ref.at[j], w_sem.at[j]).start()
-    pltpu.make_async_copy(wo_hbm, wo_ref, w_sem.at[3]).start()
+
+    @pl.when(is_hub)
+    def _():
+        wo_whole.start()
+
 
     wide = tok_ref[...].astype(F32)
     center = jnp.mean(wide, axis=-1, keepdims=True)
@@ -494,6 +514,45 @@
 
     def a_left(o):
         return line_copy(mod, o, sa_l, ra, -1)
+
+    def drain(ref, sem):
+        pltpu.make_async_copy(ref, ref, sem).wait()
+
+    def rows_of(origin, part):
+        return pl.ds(pl.multiple_of(origin * slice_rows + part * part_rows, 16), part_rows)
+
+    def origin_of(mask):
+        return b + sum((1 - 2 * ((b // bit) % 2)) * bit for bit in bits if mask & bit)
+
+    def wz_copy(part, slot):
+        return pltpu.make_async_remote_copy(
+            src_ref=wo_ref.at[rows_of(b, part)], dst_ref=wx_ref.at[slot, rows_of(b, part)],
+            send_sem=swz.at[part], recv_sem=rwz.at[slot, part],
+            device_id={"ulysses": hub}, device_id_type=MESH,
+        )
+
+    def w_copy(mask, part):
+        slot, bit = source_slot(mask, part)
+        ref = wx_ref.at[:, rows_of(origin_of(slot), part)]
+        return pltpu.make_async_remote_copy(
+            src_ref=ref, dst_ref=ref,
+            send_sem=sw, recv_sem=rw_core if mask & 1 else rw.at[mask // 2, part],
+            device_id={"blk": flip(bit)}, device_id_type=MESH,
+        )
+
+    def w_wait(mask, part):
+        ref = wx_ref.at[:, rows_of(origin_of(mask), part)]
+        pltpu.make_async_remote_copy(
+            src_ref=ref, dst_ref=ref,
+            send_sem=sw, recv_sem=rw.at[mask // 2, part],
+            device_id={"blk": flip(source_slot(mask, part)[1])}, device_id_type=MESH,
+        ).wait_recv()
+
+    def w_relay(mask, part):
+        w_wait(mask, part)
+        for later in sorted(masks, key=lambda m: m & 1):
+            if source_slot(later, part)[0] == mask:
+                w_copy(later, part).start()
 
     def source(mask, part):
         if mask & 1:
@@ -504,20 +563,31 @@
         bit = highest_bit(rest) if part == 0 else lowest_bit(rest)
         return mask - bit, bit
 
+    def b_sem(mask, part, u):
+        return rb_core if mask & 1 else rb.at[mask // 2, part, u]
+
     def b_copy(mask, part, u):
         slot, bit = source(mask, part)
         own = pl.ds(theirs if bit == SPLIT else mine, share)
         return pltpu.make_async_remote_copy(
             src_ref=kv.at[part, own, slot, u], dst_ref=kv.at[part, own, mask, u],
-            send_sem=sb.at[mask, part, u], recv_sem=rb.at[mask, part, u],
+            send_sem=sb, recv_sem=b_sem(mask, part, u),
             device_id={"blk": flip(bit)}, device_id_type=MESH,
+        )
+
+    def b_cross(bit, part, u):
+        own = pl.ds(theirs, share)
+        return pltpu.make_async_remote_copy(
+            src_ref=kv.at[part, own, 0, u], dst_ref=kv.at[part, own, SPLIT + bit, u],
+            send_sem=sb, recv_sem=b_sem(SPLIT + bit, part, u),
+            device_id={"blk": origin_of(SPLIT + bit)}, device_id_type=MESH,
         )
 
     def b_wait(mask, part, u):
         here = kv.at[part, pl.ds(mine, share), mask, u]
         pltpu.make_async_remote_copy(
             src_ref=here, dst_ref=here,
-            send_sem=sb.at[mask, part, u], recv_sem=rb.at[mask, part, u],
+            send_sem=sb, recv_sem=b_sem(mask, part, u),
             device_id={"blk": flip(source(mask, part)[1])}, device_id_type=MESH,
         ).wait_recv()
 
@@ -525,24 +595,28 @@
         heads_of = pl.ds(first, share)
         return pltpu.make_async_remote_copy(
             src_ref=q_ref.at[heads_of, 0, u], dst_ref=q_ref.at[heads_of, 1, u],
-            send_sem=sq.at[u], recv_sem=rq.at[u],
+            send_sem=sq, recv_sem=rq,
             device_id={"blk": flip(SPLIT)}, device_id_type=MESH,
         )
 
-    def b_send(slot, part, u):
+    def b_send(slot, part, u, cross=False):
         for mask in sorted(masks, key=lambda m: (m & 1, m != SPLIT)):
-            if source(mask, part)[0] == slot:
+            at, bit = source(mask, part)
+            if at == slot and not (cross and slot == SPLIT and bit != 1):
                 b_copy(mask, part, u).start()
+                if cross and mask == SPLIT:
+                    for far_bit in bits[2:]:
+                        b_cross(far_bit, part, u).start()
 
     def depth_of(mask):
         return bin(mask).count("1")
 
-    def b_level(level, u, parts=(0, 1)):
-        for part in parts:
+    def b_level(level, u, cross=False):
+        for part in (0, 1):
             for mask in masks:
                 if mask % 2 == 0 and depth_of(mask) == level:
                     b_wait(mask, part, u)
-                    b_send(mask, part, u)
+                    b_send(mask, part, u, cross)
 
     depth = len(bits) - 1
 
@@ -559,7 +633,7 @@
         meansq = jnp.mean(sums * sums, axis=-1, keepdims=True)
         return sums * lax.rsqrt(meansq + 1e-06) * gain * scale
 
-    def project(starts, count, own=False, between=None):
+    def project(starts, count, own=False, between=None, cross=False):
         size = count * half
 
         def sums_of(j):
@@ -584,12 +658,12 @@
             def put_keys(units, part):
                 kv[0, h, 0, units] = part
             put(head_norm(sums, kg_ref[...], 1.0).astype(BF), put_keys)
-        send(lambda u: b_send(0, 0, u))
+        send(lambda u: b_send(0, 0, u, cross))
         for h, sums in enumerate(sums_of(2)):
             def put_values(units, part):
                 kv[1, h, 0, units] = part
             put(sums.astype(BF), put_values)
-        send(lambda u: b_send(0, 1, u))
+        send(lambda u: b_send(0, 1, u, cross))
         if between is not None:
             between()
         for h, sums in enumerate(sums_of(0)):
@@ -607,6 +681,12 @@
         def _():
             a_left(2 * z + u).start()
 
+    @pl.when(jnp.logical_not(is_hub))
+    def _():
+        wo_slice.wait()
+        for part in range(2):
+            wz_copy(part, away - 1).start()
+
     def receive(k, u):
         @pl.when(z - k >= 0)
         def _():
@@ -652,13 +732,18 @@
         receive(1, 1)
 
     def line_step(k, _):
+        def between():
+            @pl.when(k + 1 < last)
+            def _():
+                at_each(k - 1, level_rest)
+
         with jax.named_scope("project"):
-            project_at(k, lambda: at_each(k - 1, level_rest))
+            project_at(k, between)
         receive(k + 1, 0)
-        at_each(k, level_one)
 
         @pl.when(k + 1 < last)
         def _():
+            at_each(k, level_one)
             receive(k + 1, 1)
 
         return 0
@@ -669,9 +754,25 @@
     ends = (z == 0) | (z == last)
     far = last - z
 
+    first_part = [(SPLIT, 0), (1, 0), (1, 1)]
+    direct = [
+        (mask, part) for part in (1, 0) for mask in masks
+        if mask % 2 == 0 and mask != SPLIT and source_slot(mask, part)[0] == 0
+    ]
+
+    @pl.when(is_hub)
+    def _():
+        for part in range(2):
+            for slot in range(line_half - 1):
+                wz_copy(part, slot).wait_recv()
+        for mask, part in first_part:
+            w_copy(mask, part).start()
+
     with jax.named_scope("far"):
         @pl.when(jnp.logical_not(ends))
         def _():
+            at_each(last - 1, level_one)
+            at_each(last - 2, level_rest)
             at_each(last - 1, level_rest)
 
         def far_step(u, _):
@@ -682,93 +783,64 @@
             def between():
                 @pl.when(u == 0)
                 def _():
-                    at_each(last - 1, level_rest)
-
-                @pl.when(u == 1)
-                def _():
-                    b_level(1, 2 * far)
+                    at_each(last - 1, level_one)
 
             with jax.named_scope("project_half"):
-                project([2 * far + u], 1, between=between)
+                project([2 * far + u], 1, between=between, cross=True)
             return 0
 
         @pl.when(ends)
         def _():
             lax.fori_loop(0, 2, far_step, 0)
-            b_level(1, 2 * far + 1)
+            at_each(last - 2, level_rest)
+            b_level(1, 2 * far, cross=True)
+            at_each(last - 1, level_rest)
+            b_level(1, 2 * far + 1, cross=True)
             for level in range(2, depth + 1):
-                b_level(level, 2 * far)
-                b_level(level, 2 * far + 1)
-
-    def b_finish(u, _):
-        for part in (0, 1):
-            for mask in masks:
-                if mask % 2 == 1:
-                    b_wait(mask, part, u)
-        q_copy(u, mine).wait_recv()
-        return 0
+                b_level(level, 2 * far, cross=True)
+                b_level(level, 2 * far + 1, cross=True)
+
+    @pl.when(is_hub)
+    def _():
+        for mask, part in direct:
+            w_copy(mask, part).start()
 
     with jax.named_scope("b_finish"):
-        lax.fori_loop(0, 2 * n_u, b_finish, 0)
-        pltpu.make_async_copy(wo_hbm, wo_ref, w_sem.at[3]).wait()
+        drain(kv.at[:, pl.ds(0, share), pl.ds(0, n_blk // 2)], rb_core)
+        drain(q_ref.at[pl.ds(0, share), 0], rq)
 
     keys_all = n_blk * n_u * rows
 
     def order(i, rightward):
-        inner = n_u - 2
-        low_end = (i == inner) == rightward
-        return jnp.where(i < inner, i + 1, jnp.where(low_end, 0, last))
-
-    def c_copy(o, src, sd, send, step):
+        leftward = jnp.where(i < line_half, last - i, i - line_half)
+        return jnp.where(rightward, last - leftward, leftward)
+
+    def c_copy(o, src, sd):
         ref = att.at[o, src, :, pl.ds(pl.multiple_of(sd * cols, head), cols)]
         return pltpu.make_async_remote_copy(
             src_ref=ref, dst_ref=ref,
-            send_sem=send.at[o, src, sd], recv_sem=rc.at[o, src, sd],
-            device_id={"ulysses": z + step}, device_id_type=MESH,
-        )
-
-    def c_right(o, src, sd):
-        return c_copy(o, src, sd, sc_r, 1)
-
-    def c_left(o, src, sd):
-        return c_copy(o, src, sd, sc_l, -1)
-
-    low = z < n_u // 2
+            send_sem=sc.at[src], recv_sem=rc.at[o, src, sd],
+            device_id={"ulysses": z + onward}, device_id_type=MESH,
+        )
 
     def c_send(t, sd):
-        o = order(t, low)
-
-        def start(right, chunk):
-            @pl.when(right & (z < last))
-            def _():
-                c_right(chunk, z, sd).start()
-
-            @pl.when(jnp.logical_not(right) & (z > 0))
-            def _():
-                c_left(chunk, z, sd).start()
-
-        start(low, o)
-
-        @pl.when(t != n_u - 2)
-        def _():
-            start(jnp.logical_not(low), o)
-
-        @pl.when(t == n_u - 1)
-        def _():
-            start(jnp.logical_not(low), order(t - 1, low))
+        c_copy(order(t, low), z, sd).start()
 
     def x_copy(o, sd):
         return pltpu.make_async_remote_copy(
             src_ref=xatt.at[o],
             dst_ref=att.at[o, z, :, pl.ds(pl.multiple_of(sd * cols, head), cols)],
-            send_sem=sx.at[o], recv_sem=rx.at[o],
+            send_sem=sx, recv_sem=rx.at[o],
             device_id={"blk": flip(SPLIT)}, device_id_type=MESH,
         )
 
-    def d_copy(o, src):
-        return pltpu.make_async_remote_copy(
-            src_ref=stage.at[o], dst_ref=br.at[src],
-            send_sem=sd.at[o], recv_sem=rd.at[src],
+    def quarter(d):
+        return hub - onward * d
+
+    def d_copy(o, d):
+        return pltpu.make_async_remote_copy(
+            src_ref=stage.at[o, d], dst_ref=br.at[quarter(d)],
+            send_sem=sd, recv_sem=rd.at[quarter(d)],
             device_id={"ulysses": o}, device_id_type=MESH,
         )
 
@@ -812,22 +884,21 @@
         def _():
             c_send(t, side)
 
-    def pass_on(right, o, src, sd):
-        copy = c_right(o, src, sd) if right else c_left(o, src, sd)
-        copy.wait_recv()
-
-        @pl.when((z < last) if right else (z > 0))
-        def _():
+    def pass_on(i, k):
+        src = z - onward * k
+        there = (src >= 0) & (src <= last)
+
+        @pl.when(there & (i >= 0) & (i < n_u))
+        def _():
+            copy = c_copy(order(i, low), src, side)
+            copy.wait_recv()
             copy.start()
 
-    def pass_when(when, right, i, src):
-        @pl.when(when & (i >= 0) & (i < n_u))
-        def _():
-            pass_on(right, order(i, right), src, side)
-
-        @pl.when(when & (i >= 1) & (i <= n_u))
-        def _():
-            pass_on(right, order(i - 1, right), src, 1 - side)
+        @pl.when(there & (i >= 1) & (i <= n_u))
+        def _():
+            copy = c_copy(order(i - 1, low), src, 1 - side)
+            copy.wait_recv()
+            copy.start()
 
     def x_step(t):
         x_copy(order(t, low), 1 - side).wait_recv()
@@ -837,6 +908,10 @@
         with jax.named_scope("attend"):
             attend(t)
 
+        @pl.when(is_hub & (t == n_u - 2))
+        def _():
+            w_copy(SPLIT, 1).start()
+
         @pl.when(t > 1)
         def _():
             x_step(t - 2)
@@ -845,65 +920,100 @@
 
     with jax.named_scope("attend_loop"):
         lax.fori_loop(0, n_u, attend_step, 0)
+
         for t in range(max(n_u - 2, 0), n_u):
             x_step(t)
 
-    def near_step(i, _):
-        pass_when(low & (z > 0), False, i, z + 1)
-        pass_when(jnp.logical_not(low) & (z < last), True, i, z - 1)
-        return 0
-
-    with jax.named_scope("near_loop"):
-        lax.fori_loop(0, n_u + 1, near_step, 0)
-
-    gap = 2
-    reach = jnp.where(ends, last, jnp.maximum(z, last - z))
-
-    def mix(i, _):
-        o = order(i, jnp.logical_not(low))
+        @pl.when(is_hub)
+        def _():
+            w_relay(SPLIT, 0)
+            w_relay(2 * SPLIT, 1)
+
+    def mix(indices, weights, d):
+        chunks = [order(i, jnp.logical_not(low)) for i in indices]
         with jax.named_scope("mix"):
-            total = jnp.zeros((rows, width), F32)
+            total = jnp.zeros((len(chunks) * rows, width), F32)
             for src in range(n_u):
                 total += jnp.dot(
-                    att[o, src], wo_ref[src * width:(src + 1) * width, :],
+                    jnp.concatenate([att[o, src] for o in chunks], axis=0),
+                    weights[src * width:(src + 1) * width, :],
                     preferred_element_type=F32,
                 )
-
-        @pl.when(o == z)
-        def _():
-            br[z] = total.astype(BF)
-
-        @pl.when(o != z)
-        def _():
-            stage[o] = total.astype(BF)
-            d_copy(o, z).start()
+            result = total.astype(BF)
+        for g, o in enumerate(chunks):
+            part = result[g * rows:(g + 1) * rows]
+
+            @pl.when(o == z)
+            def _():
+                br[quarter(d)] = part
+
+            @pl.when(o != z)
+            def _():
+                stage[o, d] = part
+                d_copy(o, d).start()
+
+    def gathered(i):
+        for k in range(line_half):
+            for sd_of in (side, 1 - side):
+                c_copy(order(i, jnp.logical_not(low)), hub + onward * (k + 1), sd_of).wait_recv()
+
+    gap = 2
+    steps = n_u + 1 + gap * (line_half - 2)
+
+    def pass_step(t, _):
+        for k in range(1, line_half):
+            pass_on(t - gap * (k - 1), k)
+
+        @pl.when(is_hub & (t == 1))
+        def _():
+            w_relay(SPLIT, 1)
+            w_relay(2 * SPLIT, 0)
+
+        i = t - (steps - line_half)
+
+        @pl.when(is_hub & (i >= 0))
+        def _():
+            gathered(i)
+            mix([i], wo_ref, 0)
 
         return 0
 
-    def mix_step(t, _):
-        for k in range(1, last + 1):
-            i = t - gap * (k - 1)
-            if k == 1:
-                pass_when((z >= k) & (low | (z == last)), True, i, z - k)
-                pass_when((z + k <= last) & (jnp.logical_not(low) | (z == 0)), False, i, z + k)
-            else:
-                pass_when(z >= k, True, i, z - k)
-                pass_when(z + k <= last, False, i, z + k)
-
-        i = t - gap * (reach - 1) - 1
-        held = (i >= 0) & (i < n_u) & (ends | (i != n_u - 2))
-        both = jnp.logical_not(ends) & (i == n_u - 1)
-        lax.fori_loop(jnp.where(both, i - 1, i), jnp.where(held, i + 1, i), mix, 0)
-        return 0
-
-    with jax.named_scope("mix_loop"):
-        lax.fori_loop(0, n_u + gap * (last - 1) + 1, mix_step, 0)
+    with jax.named_scope("pass_loop"):
+        @pl.when(is_hub)
+        def _():
+            wo_whole.wait()
+
+        lax.fori_loop(0, steps, pass_step, 0)
+
+    with jax.named_scope("hub"):
+        @pl.when(is_hub)
+        def _():
+            with jax.named_scope("w_last"):
+                for mask in sorted(masks, key=depth_of):
+                    if mask % 2 == 0 and mask not in (SPLIT, 2 * SPLIT):
+                        for part in range(2):
+                            w_relay(mask, part)
+                drain(wx_ref.at[:, pl.ds(0, n_blk // 2 * slice_rows)], rw_core)
+
+            first, second = range(line_half), range(line_half, n_u)
+            for d in range(1, line_half):
+                mix(first, wx_ref.at[d - 1], d)
+            for group in ([i for i in second[:-1]], [n_u - 1]):
+                for i in group:
+                    gathered(i)
+                mix(group, wo_ref, 0)
+                for d in range(1, line_half):
+                    mix(group, wx_ref.at[d - 1], d)
 
     with jax.named_scope("final"):
         for src in range(n_u):
-            @pl.when(src != z)
-            def _():
-                d_copy(src, src).wait_recv()
+            @pl.when(jnp.logical_not(is_hub) | (low != (src < line_half)))
+            def _():
+                pltpu.make_async_remote_copy(
+                    src_ref=br.at[src], dst_ref=br.at[src],
+                    send_sem=rd.at[src], recv_sem=rd.at[src],
+                    device_id={"ulysses": last - hub}, device_id_type=MESH,
+                ).wait_recv()
 
             at = slice(src * width, (src + 1) * width)
             out_ref[:, at] = (
@@ -920,31 +1030,28 @@
             def _():
                 a_left(2 * s + u).wait_send()
 
-        for src in range(n_u):
-            for sd_of in range(2):
-                @pl.when((src <= z) & (z < last))
-                def _():
-                    c_right(s, src, sd_of).wait_send()
-
-                @pl.when((src >= z) & (z > 0))
-                def _():
-                    c_left(s, src, sd_of).wait_send()
-
-        @pl.when(s != z)
-        def _():
-            d_copy(s, z).wait_send()
-
-        x_copy(s, side).wait_send()
-        for u in range(2):
-            q_copy(2 * s + u, theirs).wait_send()
-        for part in (0, 1):
-            for mask in masks:
-                for u in range(2):
-                    b_copy(mask, part, 2 * s + u).wait_send()
+        @pl.when(jnp.where(low, s <= z, s >= z))
+        def _():
+            drain(att.at[:, s], sc.at[s])
+
         return 0
 
     with jax.named_scope("finish"):
         lax.fori_loop(0, n_u, finish, 0)
+
+        drain(xatt, sx)
+        drain(q_ref.at[pl.ds(0, share), 0], sq)
+        drain(kv.at[:, pl.ds(0, share), pl.ds(1, n_blk - 1)], sb)
+
+        @pl.when(is_hub)
+        def _():
+            drain(stage.at[pl.ds(0, n_u - 1)], sd)
+            drain(wx_ref.at[:, pl.ds(0, (n_blk - 1) * slice_rows)], sw)
+
+        @pl.when(jnp.logical_not(is_hub))
+        def _():
+            for part in range(2):
+                wz_copy(part, away - 1).wait_send()
 
 
 def local(n_u, n_blk, tokens, mod_shift, mod_scale, mod_gate, qkv_weight, query_gain, key_gain, out_weight):
@@ -953,9 +1060,9 @@
     head = query_gain.shape[0]
     heads = width // head
     vmem = pl.BlockSpec(memory_space=pltpu.VMEM)
-    hbm = pl.BlockSpec(memory_space=pl.ANY)
+    hbm = pl.BlockSpec(memory_space=pltpu.HBM)
     dma = pltpu.SemaphoreType.DMA
-    split = heads % 2 == 0 and n_blk % (2 * SPLIT) == 0
+    split = heads % 2 == 0 and n_blk % (2 * SPLIT) == 0 and n_u % 2 == 0 and n_u > 2
     buffers = [
         pltpu.VMEM(qkv_weight.shape, BF),
         pltpu.VMEM(out_weight.shape, BF),
@@ -968,17 +1075,20 @@
     mixed = pltpu.VMEM((n_u, rows, width), BF)
     row = pltpu.VMEM((1, model), F32)
     early = hbm if split else vmem
+    one = pltpu.SemaphoreType.DMA
     if split:
         body = split_kernel
         scratch = buffers + [
             pltpu.VMEM((heads, 2, 2 * n_u, rows // 2, head), BF), keys,
+            pltpu.VMEM((n_u // 2 - 1, *out_weight.shape), BF),
             attended, pltpu.VMEM((n_u, rows, width // 2), BF),
-            pltpu.VMEM((2 * rows, width // 2), BF), mixed, mixed,
+            pltpu.VMEM((2 * rows, width // 2), BF),
+            pltpu.VMEM((n_u, n_u // 2, rows, width), BF), mixed,
             pltpu.VMEM((rows, model), BF), row, row, row, dma((4,)),
-        ] + line_sems + block_sems + [
-            dma((2 * n_u,)), dma((2 * n_u,)), dma((n_u,)), dma((n_u,)),
-            dma((n_u, n_u, 2)), dma((n_u, n_u, 2)), dma((n_u, n_u, 2)),
-            dma((n_u,)), dma((n_u,)),
+            dma((2,)), dma((n_u // 2 - 1, 2)), one, dma((n_blk // 2, 2)), one,
+        ] + line_sems + [
+            one, dma((n_blk // 2, 2, 2 * n_u)), one, one, one, one, dma((n_u,)),
+            dma((n_u,)), dma((n_u, n_u, 2)), one, dma((n_u,)),
         ]
     else:
         body = kernel
@@ -991,12 +1101,12 @@
         ]
     return pl.pallas_call(
         functools.partial(body, n_u, n_blk),
-        out_shape=jax.ShapeDtypeStruct((rows, model), BF),
+        out_shape=pltpu.VMEM((rows, model), BF) if split else jax.ShapeDtypeStruct((rows, model), BF),
         in_specs=[early, early, early, early, hbm, vmem, vmem, hbm],
         out_specs=vmem,
         scratch_shapes=scratch,
         compiler_params=pltpu.CompilerParams(
-            collective_id=0, has_side_effects=True, vmem_limit_bytes=66_000_000
+            collective_id=0, has_side_effects=True, vmem_limit_bytes=63_000_000 if split else 66_000_000
         ),
     )(
         tokens, mod_shift[None], mod_scale[None], mod_gate[None],

time: 80.3 us -> 70.6 us (0.88)
  Pallas kernels: 78.3 us -> 69.7 us
  local copies, waits for them, and re-layouts: 1.77 us -> 0.75 us
    pallas_call x1, Pallas kernels: 78.3 us -> 69.7 us  [local(): pl.pallas_call(functools.partial(body, n_u, n_blk), out_shape=pltpu.VMEM(...]
    unnamed x1, local copies, waits for them, and re-layouts: 1.77 us -> 0.75 us
where the time goes in v3:
time: 70.6 us; the launch traced here: 70.4 us
  Pallas kernels  69.7 us (99%)
  local copies, waits for them, and re-layouts  0.75 us (1%)
    pallas_call x1, Pallas kernels, local(): pl.pallas_call(functools.partial(body, n_u, n_blk), out_shape=pltpu.VMEM(...  69.7 us

profile of v3, /device:TPU:0, one launch (start us, length us, event | category | flops | bytes accessed | tf_op | source)
XLA Modules:
  0.0 70.4 jit_solution(7753590896411219921)
XLA Ops:
  0.0 69.7 %shard_map.82 = bf16[64,3072]{1,0:T(8,128)(2,1)S(1)} custom-call(bf16[64,3072]{1,0:T(8,128)(2,1)} %tok_hbm.1, f32[1,3072]{1,0:T(1,128)} %bitcast.5, f32[1,3072]{1,0:T(1,128)} %bitcast.6, f32[1,3072]{1,0:T(1,128)} %bitcast.7, bf16[3,3072,768]{2,1,0:T(8,128)(2,1)} %w_hbm.1, f32[1,128]{1,0:T(1,128)} %bitcast.8, f32[1,128]{1,0:T(1,128)} %bitcast.9, ...), custom_call_target="tpu_custom_call" | custom-call | tf_op jit(solution)/shard_map/pallas_call | solution.py:1102
  69.7 0.7 %copy.10 = bf16[64,3072]{1,0:T(8,128)(2,1)} copy(bf16[64,3072]{1,0:T(8,128)(2,1)S(1)} %shard_map.82) | data formatting | bytes 786432

commit v4 on v3

--- a/solution.py
+++ b/solution.py
@@ -12,6 +12,7 @@
 BF = jnp.bfloat16
 F32 = jnp.float32
 SPLIT = 2
+Z_MASKS = (0, 3 * SPLIT)
 
 
 def highest_bit(mask):
@@ -426,7 +427,7 @@
 def split_kernel(
     n_u, n_blk,
     tok_hbm, shift_hbm, scale_hbm, gate_hbm, w_hbm, qg_ref, kg_ref, wo_hbm, out_ref,
-    w_ref, wo_ref, mod, q_ref, kv, wx_ref, att, xatt, pair_ref, stage, br,
+    w_ref, wo_ref, mod, q_ref, kv, wx_ref, att, xatt, stage, br,
     tok_ref, shift_ref, scale_ref, gate_ref, in_sem, swz, rwz, sw, rw, rw_core,
     w_sem, sa_r, sa_l, ra, sb, rb, rb_core, sq, rq, sx, rx, sc, rc, sd, rd,
 ):
@@ -476,13 +477,22 @@
         copy.start()
     for copy in inputs:
         copy.wait()
-    own_slice = pl.ds(pl.multiple_of(b * slice_rows, 16), slice_rows)
-    wo_slice = pltpu.make_async_copy(wo_hbm.at[own_slice], wo_ref.at[own_slice], w_sem.at[3])
+    def origin_of(mask):
+        return b + sum((1 - 2 * ((b // bit) % 2)) * bit for bit in bits if mask & bit)
+
+    slices = [
+        pl.ds(pl.multiple_of(origin_of(mask) * slice_rows, 16), slice_rows) for mask in Z_MASKS
+    ]
+    wo_slices = [
+        pltpu.make_async_copy(wo_hbm.at[rows_at], wo_ref.at[rows_at], w_sem.at[3 + i])
+        for i, rows_at in enumerate(slices)
+    ]
     wo_whole = pltpu.make_async_copy(wo_hbm, wo_ref, w_sem.at[3])
 
     @pl.when(jnp.logical_not(is_hub))
     def _():
-        wo_slice.start()
+        for copy in wo_slices:
+            copy.start()
 
     for j in (1, 2, 0):
         pltpu.make_async_copy(w_hbm.at[j], w_ref.at[j], w_sem.at[j]).start()
@@ -521,13 +531,12 @@
     def rows_of(origin, part):
         return pl.ds(pl.multiple_of(origin * slice_rows + part * part_rows, 16), part_rows)
 
-    def origin_of(mask):
-        return b + sum((1 - 2 * ((b // bit) % 2)) * bit for bit in bits if mask & bit)
-
-    def wz_copy(part, slot):
-        return pltpu.make_async_remote_copy(
-            src_ref=wo_ref.at[rows_of(b, part)], dst_ref=wx_ref.at[slot, rows_of(b, part)],
-            send_sem=swz.at[part], recv_sem=rwz.at[slot, part],
+    def wz_copy(i, part, slot):
+        origin = origin_of(Z_MASKS[i])
+        return pltpu.make_async_remote_copy(
+            src_ref=wo_ref.at[rows_of(origin, part)],
+            dst_ref=wx_ref.at[slot, rows_of(origin, part)],
+            send_sem=swz.at[i, part], recv_sem=rwz.at[slot, i, part],
             device_id={"ulysses": hub}, device_id_type=MESH,
         )
 
@@ -548,11 +557,18 @@
             device_id={"blk": flip(source_slot(mask, part)[1])}, device_id_type=MESH,
         ).wait_recv()
 
+    def w_onward(mask, part):
+        for later in sorted(masks, key=lambda m: m & 1):
+            if source_slot(later, part)[0] == mask and later not in Z_MASKS:
+                w_copy(later, part).start()
+
     def w_relay(mask, part):
         w_wait(mask, part)
-        for later in sorted(masks, key=lambda m: m & 1):
-            if source_slot(later, part)[0] == mask:
-                w_copy(later, part).start()
+        w_onward(mask, part)
+
+    def w_arrived(i, part):
+        for slot in range(line_half - 1):
+            wz_copy(i, part, slot).wait_recv()
 
     def source(mask, part):
         if mask & 1:
@@ -564,7 +580,7 @@
         return mask - bit, bit
 
     def b_sem(mask, part, u):
-        return rb_core if mask & 1 else rb.at[mask // 2, part, u]
+        return rb_core if mask & 1 else rb.at[mask // 2 - 1, part, u]
 
     def b_copy(mask, part, u):
         slot, bit = source(mask, part)
@@ -683,9 +699,10 @@
 
     @pl.when(jnp.logical_not(is_hub))
     def _():
-        wo_slice.wait()
-        for part in range(2):
-            wz_copy(part, away - 1).start()
+        for i, copy in enumerate(wo_slices):
+            copy.wait()
+            for part in range(2):
+                wz_copy(i, part, away - 1).start()
 
     def receive(k, u):
         @pl.when(z - k >= 0)
@@ -763,8 +780,7 @@
     @pl.when(is_hub)
     def _():
         for part in range(2):
-            for slot in range(line_half - 1):
-                wz_copy(part, slot).wait_recv()
+            w_arrived(0, part)
         for mask, part in first_part:
             w_copy(mask, part).start()
 
@@ -845,44 +861,26 @@
         )
 
     def attend(t):
-        first, second = t == 0, t == n_u - 1
-        groups = (
-            (first, order(jnp.where(first, 0, t - 1), low)),
-            (jnp.logical_not(second), order(jnp.where(second, t, t + 1), low)),
-        )
+        o = order(t, low)
+        place = pl.multiple_of(side * cols, head)
         for r in range(share):
             h = mine + r
             keys = kv[0, h].reshape(keys_all, head)
             values = kv[1, h].reshape(keys_all, head)
-            queries = jnp.concatenate([
-                q_ref[h, jnp.where(away, 1, 0), pl.ds(2 * o, 2)].reshape(rows, head)
-                for away, o in groups
-            ], axis=0)
+            queries = jnp.concatenate(
+                [q_ref[h, p, pl.ds(2 * o, 2)].reshape(rows, head) for p in range(2)], axis=0
+            )
             scores = lax.dot_general(
                 queries, keys, (((1,), (1,)), ((), ())), preferred_element_type=F32
             )
             powers = jnp.exp(scores - jnp.max(scores, axis=-1, keepdims=True))
             total = jnp.sum(powers, axis=-1, keepdims=True)
             numerator = jnp.dot(powers.astype(BF), values, preferred_element_type=F32)
-            pair_ref[:, r * head:(r + 1) * head] = (numerator / total).astype(BF)
-        for g, (away, o) in enumerate(groups):
-            @pl.when(away)
-            def _():
-                xatt[o] = pair_ref[g * rows:(g + 1) * rows]
-                x_copy(o, side).start()
-
-            @pl.when(jnp.logical_not(away))
-            def _():
-                place = pl.ds(pl.multiple_of(side * cols, head), cols)
-                att[o, z, :, place] = pair_ref[g * rows:(g + 1) * rows]
-
-        @pl.when(t > 0)
-        def _():
-            c_send(t - 1, side)
-
-        @pl.when(second)
-        def _():
-            c_send(t, side)
+            result = (numerator / total).astype(BF)
+            att[o, z, :, pl.ds(pl.multiple_of(place + r * head, head), head)] = result[:rows]
+            xatt[o, :, r * head:(r + 1) * head] = result[rows:]
+        x_copy(o, side).start()
+        c_send(t, side)
 
     def pass_on(i, k):
         src = z - onward * k
@@ -908,7 +906,7 @@
         with jax.named_scope("attend"):
             attend(t)
 
-        @pl.when(is_hub & (t == n_u - 2))
+        @pl.when(is_hub & (t == n_u - 1))
         def _():
             w_copy(SPLIT, 1).start()
 
@@ -928,6 +926,9 @@
         def _():
             w_relay(SPLIT, 0)
             w_relay(2 * SPLIT, 1)
+            for part in range(2):
+                w_arrived(1, part)
+                w_onward(Z_MASKS[1], part)
 
     def mix(indices, weights, d):
         chunks = [order(i, jnp.logical_not(low)) for i in indices]
@@ -964,7 +965,7 @@
         for k in range(1, line_half):
             pass_on(t - gap * (k - 1), k)
 
-        @pl.when(is_hub & (t == 1))
+        @pl.when(is_hub & (t == 2))
         def _():
             w_relay(SPLIT, 1)
             w_relay(2 * SPLIT, 0)
@@ -990,20 +991,22 @@
         def _():
             with jax.named_scope("w_last"):
                 for mask in sorted(masks, key=depth_of):
-                    if mask % 2 == 0 and mask not in (SPLIT, 2 * SPLIT):
+                    if mask % 2 == 0 and mask not in (SPLIT, 2 * SPLIT, *Z_MASKS):
                         for part in range(2):
                             w_relay(mask, part)
                 drain(wx_ref.at[:, pl.ds(0, n_blk // 2 * slice_rows)], rw_core)
 
-            first, second = range(line_half), range(line_half, n_u)
             for d in range(1, line_half):
-                mix(first, wx_ref.at[d - 1], d)
-            for group in ([i for i in second[:-1]], [n_u - 1]):
-                for i in group:
-                    gathered(i)
-                mix(group, wo_ref, 0)
+                mix(range(line_half), wx_ref.at[d - 1], d)
+
+            def near_mix(i, _):
+                gathered(i)
+                mix([i], wo_ref, 0)
                 for d in range(1, line_half):
-                    mix(group, wx_ref.at[d - 1], d)
+                    mix([i], wx_ref.at[d - 1], d)
+                return 0
+
+            lax.fori_loop(line_half, n_u, near_mix, 0)
 
     with jax.named_scope("final"):
         for src in range(n_u):
@@ -1046,12 +1049,13 @@
         @pl.when(is_hub)
         def _():
             drain(stage.at[pl.ds(0, n_u - 1)], sd)
-            drain(wx_ref.at[:, pl.ds(0, (n_blk - 1) * slice_rows)], sw)
+            drain(wx_ref.at[:, pl.ds(0, (n_blk - len(Z_MASKS)) * slice_rows)], sw)
 
         @pl.when(jnp.logical_not(is_hub))
         def _():
-            for part in range(2):
-                wz_copy(part, away - 1).wait_send()
+            for i in range(len(Z_MASKS)):
+                for part in range(2):
+                    wz_copy(i, part, away - 1).wait_send()
 
 
 def local(n_u, n_blk, tokens, mod_shift, mod_scale, mod_gate, qkv_weight, query_gain, key_gain, out_weight):
@@ -1062,7 +1066,7 @@
     vmem = pl.BlockSpec(memory_space=pltpu.VMEM)
     hbm = pl.BlockSpec(memory_space=pltpu.HBM)
     dma = pltpu.SemaphoreType.DMA
-    split = heads % 2 == 0 and n_blk % (2 * SPLIT) == 0 and n_u % 2 == 0 and n_u > 2
+    split = heads % 2 == 0 and n_blk % (4 * SPLIT) == 0 and n_u % 2 == 0 and n_u > 2
     buffers = [
         pltpu.VMEM(qkv_weight.shape, BF),
         pltpu.VMEM(out_weight.shape, BF),
@@ -1082,12 +1086,12 @@
             pltpu.VMEM((heads, 2, 2 * n_u, rows // 2, head), BF), keys,
             pltpu.VMEM((n_u // 2 - 1, *out_weight.shape), BF),
             attended, pltpu.VMEM((n_u, rows, width // 2), BF),
-            pltpu.VMEM((2 * rows, width // 2), BF),
             pltpu.VMEM((n_u, n_u // 2, rows, width), BF), mixed,
             pltpu.VMEM((rows, model), BF), row, row, row, dma((4,)),
-            dma((2,)), dma((n_u // 2 - 1, 2)), one, dma((n_blk // 2, 2)), one,
-        ] + line_sems + [
-            one, dma((n_blk // 2, 2, 2 * n_u)), one, one, one, one, dma((n_u,)),
+            dma((2, 2)), dma((n_u // 2 - 1, 2, 2)), one, dma((n_blk // 2, 2)), one,
+            dma((5,)),
+        ] + line_sems[1:] + [
+            one, dma((n_blk // 2 - 1, 2, 2 * n_u)), one, one, one, one, dma((n_u,)),
             dma((n_u,)), dma((n_u, n_u, 2)), one, dma((n_u,)),
         ]
     else:

time: 70.6 us -> 67.7 us (0.959)
  Pallas kernels: 69.7 us -> 66.8 us
    pallas_call x1, Pallas kernels: 69.7 us -> 66.8 us  [local(): pl.pallas_call(functools.partial(body, n_u, n_blk), out_shape=pltpu.VMEM(...]
where the time goes in v4:
time: 67.7 us; the launch traced here: 67.5 us
  Pallas kernels  66.8 us (99%)
  local copies, waits for them, and re-layouts  0.75 us (1%)
    pallas_call x1, Pallas kernels, local(): pl.pallas_call(functools.partial(body, n_u, n_blk), out_shape=pltpu.VMEM(...  66.8 us

profile of v4, /device:TPU:0, one launch (start us, length us, event | category | flops | bytes accessed | tf_op | source)
XLA Modules:
  0.0 67.5 jit_solution(13339516622458048952)
XLA Ops:
  0.0 66.8 %shard_map.82 = bf16[64,3072]{1,0:T(8,128)(2,1)S(1)} custom-call(bf16[64,3072]{1,0:T(8,128)(2,1)} %tok_hbm.1, f32[1,3072]{1,0:T(1,128)} %bitcast.5, f32[1,3072]{1,0:T(1,128)} %bitcast.6, f32[1,3072]{1,0:T(1,128)} %bitcast.7, bf16[3,3072,768]{2,1,0:T(8,128)(2,1)} %w_hbm.1, f32[1,128]{1,0:T(1,128)} %bitcast.8, f32[1,128]{1,0:T(1,128)} %bitcast.9, ...), custom_call_target="tpu_custom_call" | custom-call | tf_op jit(solution)/shard_map/pallas_call | solution.py:1106
  66.8 0.7 %copy.10 = bf16[64,3072]{1,0:T(8,128)(2,1)} copy(bf16[64,3072]{1,0:T(8,128)(2,1)S(1)} %shard_map.82) | data formatting | bytes 786432

commit v5 on v4

--- a/solution.py
+++ b/solution.py
@@ -579,71 +579,73 @@
         bit = highest_bit(rest) if part == 0 else lowest_bit(rest)
         return mask - bit, bit
 
-    def b_sem(mask, part, u):
-        return rb_core if mask & 1 else rb.at[mask // 2 - 1, part, u]
-
-    def b_copy(mask, part, u):
+    def b_sem(mask, part, u, count):
+        at = u // 2 if count == 2 else jnp.where(u % 2 == 0, u // 2, n_u)
+        return rb_core if mask & 1 else rb.at[mask // 2 - 1, part, at]
+
+    def b_copy(mask, part, u, count):
+        units = pl.ds(u, count)
         slot, bit = source(mask, part)
         own = pl.ds(theirs if bit == SPLIT else mine, share)
         return pltpu.make_async_remote_copy(
-            src_ref=kv.at[part, own, slot, u], dst_ref=kv.at[part, own, mask, u],
-            send_sem=sb, recv_sem=b_sem(mask, part, u),
+            src_ref=kv.at[part, own, slot, units], dst_ref=kv.at[part, own, mask, units],
+            send_sem=sb, recv_sem=b_sem(mask, part, u, count),
             device_id={"blk": flip(bit)}, device_id_type=MESH,
         )
 
-    def b_cross(bit, part, u):
+    def b_cross(bit, part, u, count):
+        units = pl.ds(u, count)
         own = pl.ds(theirs, share)
         return pltpu.make_async_remote_copy(
-            src_ref=kv.at[part, own, 0, u], dst_ref=kv.at[part, own, SPLIT + bit, u],
-            send_sem=sb, recv_sem=b_sem(SPLIT + bit, part, u),
+            src_ref=kv.at[part, own, 0, units], dst_ref=kv.at[part, own, SPLIT + bit, units],
+            send_sem=sb, recv_sem=b_sem(SPLIT + bit, part, u, count),
             device_id={"blk": origin_of(SPLIT + bit)}, device_id_type=MESH,
         )
 
-    def b_wait(mask, part, u):
-        here = kv.at[part, pl.ds(mine, share), mask, u]
+    def b_wait(mask, part, u, count):
+        here = kv.at[part, pl.ds(mine, share), mask, pl.ds(u, count)]
         pltpu.make_async_remote_copy(
             src_ref=here, dst_ref=here,
-            send_sem=sb, recv_sem=b_sem(mask, part, u),
+            send_sem=sb, recv_sem=b_sem(mask, part, u, count),
             device_id={"blk": flip(source(mask, part)[1])}, device_id_type=MESH,
         ).wait_recv()
 
-    def q_copy(u, first):
+    def q_copy(u, first, count):
         heads_of = pl.ds(first, share)
         return pltpu.make_async_remote_copy(
-            src_ref=q_ref.at[heads_of, 0, u], dst_ref=q_ref.at[heads_of, 1, u],
+            src_ref=q_ref.at[heads_of, 0, pl.ds(u, count)],
+            dst_ref=q_ref.at[heads_of, 1, pl.ds(u, count)],
             send_sem=sq, recv_sem=rq,
             device_id={"blk": flip(SPLIT)}, device_id_type=MESH,
         )
 
-    def b_send(slot, part, u, cross=False):
+    def b_send(slot, part, u, count, cross=False):
         for mask in sorted(masks, key=lambda m: (m & 1, m != SPLIT)):
             at, bit = source(mask, part)
             if at == slot and not (cross and slot == SPLIT and bit != 1):
-                b_copy(mask, part, u).start()
+                b_copy(mask, part, u, count).start()
                 if cross and mask == SPLIT:
                     for far_bit in bits[2:]:
-                        b_cross(far_bit, part, u).start()
+                        b_cross(far_bit, part, u, count).start()
 
     def depth_of(mask):
         return bin(mask).count("1")
 
-    def b_level(level, u, cross=False):
+    def b_level(level, u, count=1, cross=False):
         for part in (0, 1):
             for mask in masks:
                 if mask % 2 == 0 and depth_of(mask) == level:
-                    b_wait(mask, part, u)
-                    b_send(mask, part, u, cross)
+                    b_wait(mask, part, u, count)
+                    b_send(mask, part, u, count, cross)
 
     depth = len(bits) - 1
 
     def level_one(o):
-        for u in range(2):
-            b_level(1, 2 * o + u)
+        b_level(1, 2 * o, 2)
 
     def level_rest(o):
         for level in range(2, depth + 1):
-            for u in range(2):
-                b_level(level, 2 * o + u)
+            b_level(level, 2 * o, 2)
 
     def head_norm(sums, gain, scale):
         meansq = jnp.mean(sums * sums, axis=-1, keepdims=True)
@@ -667,26 +669,25 @@
 
         def send(act):
             for first in starts:
-                for u in range(count):
-                    act(first + u)
+                act(first)
 
         for h, sums in enumerate(sums_of(1)):
             def put_keys(units, part):
                 kv[0, h, 0, units] = part
             put(head_norm(sums, kg_ref[...], 1.0).astype(BF), put_keys)
-        send(lambda u: b_send(0, 0, u, cross))
+        send(lambda u: b_send(0, 0, u, count, cross))
         for h, sums in enumerate(sums_of(2)):
             def put_values(units, part):
                 kv[1, h, 0, units] = part
             put(sums.astype(BF), put_values)
-        send(lambda u: b_send(0, 1, u, cross))
+        send(lambda u: b_send(0, 1, u, count, cross))
         if between is not None:
             between()
         for h, sums in enumerate(sums_of(0)):
             def put_queries(units, part):
                 q_ref[h, 0, units] = part
             put(head_norm(sums, qg_ref[...], factor).astype(BF), put_queries)
-        send(lambda u: q_copy(u, theirs).start())
+        send(lambda u: q_copy(u, theirs, count).start())
 
     for u in range(2):
         @pl.when(z < last)
@@ -1091,7 +1092,7 @@
             dma((2, 2)), dma((n_u // 2 - 1, 2, 2)), one, dma((n_blk // 2, 2)), one,
             dma((5,)),
         ] + line_sems[1:] + [
-            one, dma((n_blk // 2 - 1, 2, 2 * n_u)), one, one, one, one, dma((n_u,)),
+            one, dma((n_blk // 2 - 1, 2, n_u + 1)), one, one, one, one, dma((n_u,)),
             dma((n_u,)), dma((n_u, n_u, 2)), one, dma((n_u,)),
         ]
     else:

time: 67.7 us -> 67.5 us (level)
  no operation moved by 1% of the time
where the time goes in v5:
time: 67.5 us; the launch traced here: 67.3 us
  Pallas kernels  66.6 us (99%)
  local copies, waits for them, and re-layouts  0.75 us (1%)
    pallas_call x1, Pallas kernels, local(): pl.pallas_call(functools.partial(body, n_u, n_blk), out_shape=pltpu.VMEM(...  66.6 us

profile of v5, /device:TPU:0, one launch (start us, length us, event | category | flops | bytes accessed | tf_op | source)
XLA Modules:
  0.0 67.3 jit_solution(7633501037962499723)
XLA Ops:
  0.0 66.6 %shard_map.82 = bf16[64,3072]{1,0:T(8,128)(2,1)S(1)} custom-call(bf16[64,3072]{1,0:T(8,128)(2,1)} %tok_hbm.1, f32[1,3072]{1,0:T(1,128)} %bitcast.5, f32[1,3072]{1,0:T(1,128)} %bitcast.6, f32[1,3072]{1,0:T(1,128)} %bitcast.7, bf16[3,3072,768]{2,1,0:T(8,128)(2,1)} %w_hbm.1, f32[1,128]{1,0:T(1,128)} %bitcast.8, f32[1,128]{1,0:T(1,128)} %bitcast.9, ...), custom_call_target="tpu_custom_call" | custom-call | tf_op jit(solution)/shard_map/pallas_call | solution.py:1107
  66.6 0.7 %copy.10 = bf16[64,3072]{1,0:T(8,128)(2,1)} copy(bf16[64,3072]{1,0:T(8,128)(2,1)S(1)} %shard_map.82) | data formatting | bytes 786432
